TPU v7x, 512 devices: a whole 4x4x16 slice. The times are simulated.
512 devices in a mesh: seq: 32 (over x_hi, z), head: 16 (over x_lo, y, core).
Axes of the slice: x: 4 (x_hi: 2, x_lo: 2; x = x_hi * 2 + x_lo), y: 4, z: 16, core: 2. Of those that a mesh axis runs over, the one named last changes fastest.
Arguments:
- tokens: bfloat16 [8192, 4608], P('seq', 'head'), may hold values from -32 to 32
- segments: int32 [8192], P('seq'), may hold values from 0 to 7, never falling along the last dimension, each value on 1 to 4096 neighbouring positions
- pre_gain: float32 [4608], replicated, may hold values from 0.1 to 1.9
- post_gain: float32 [4608], replicated, may hold values from 0.1 to 1.9
- w_query: bfloat16 [4608, 4096], P('seq', 'head'), may hold values from -0.375 to 0.375
- w_key: bfloat16 [4608, 2048], P('seq', 'head'), may hold values from -0.1875 to 0.1875
- w_value: bfloat16 [4608, 2048], P('seq', 'head'), may hold values from -0.09375 to 0.09375
- w_out: bfloat16 [4096, 4608], P('head', 'seq'), may hold values from -0.09375 to 0.09375
Outputs:
- mixed: bfloat16 [8192, 4608], P('seq')
Inputs may be any that keep to these rules, and one draw needn't show every extreme that they name: `segments`: segment ids never fall; each of the 8 documents holds at least one token and at most 4096, one exactly 4096.
All inputs are finite; a program needn't handle non-finite values.
Results may differ from a plain program's by a relative error of at most 0.01.
Values may be sent and summed in bfloat16 or wider, within the bound.
No kernel may reach another device: no remote copies, remote signals or barrier semaphores. Data moves between devices by JAX's collectives and lax.ppermute only.
A program may use at most 64 MiB of HBM per device.

v0:
```python
import jax
import jax.numpy as jnp
from jax import lax
from jax.sharding import Mesh
from jax.sharding import PartitionSpec as P

D = 4608
HD = 128
GROUP = 2
SCALAR = 144
DOCS = 8
SEQ = ("seq_0", "seq_1")


EPS = 1e-06
CAP = 50.0


def sent_together(arrays, axis, dim, along):
    widths = [a.shape[along] for a in arrays]
    both = jnp.concatenate(arrays, axis=along)
    filled = lax.all_gather(both, axis, axis=dim, tiled=True)
    return tuple(jnp.split(filled, [sum(widths[:k]) for k in range(1, len(widths))], axis=along))


def from_everyone(shard, axis):
    copies = jnp.broadcast_to(shard, (lax.axis_size(axis), *shard.shape))
    return lax.all_to_all(copies, axis, split_axis=0, concat_axis=0, tiled=True)


def combined_pairwise(pieces, combine):
    while len(jax.tree.leaves(pieces)[0]) > 1:
        pieces = jax.vmap(combine)(*(pieces[side::2] for side in (0, 1)))
    return pieces[0]


def entering(shard, axis, combine, identity):
    count, index = (lax.axis_size(axis), lax.axis_index(axis))
    passed = jnp.arange(count) < index

    def kept(part, zero, own):
        part = jnp.where(
            passed.reshape(-1, *(1 for _ in own.shape)), part, jnp.asarray(zero, own.dtype)
        )
        return part

    pieces = from_everyone(shard, axis)
    return combined_pairwise(kept(pieces, identity, shard), combine)


def joined_along(blocks, dim):
    lengths = list(blocks.shape[1:])
    lengths[dim] *= blocks.shape[0]
    return jnp.moveaxis(blocks, 0, dim).reshape(lengths)


def all_blocks(shard, axes, order):
    blocks = shard[None]
    for k in order:
        blocks = lax.all_gather(blocks, axes[k], axis=0, tiled=True)
    current = [lax.axis_size(axes[k]) for k in reversed(order)]
    blocks = blocks.reshape(*current, *shard.shape)
    turned = sorted(range(len(order)), key=lambda place: order[len(order) - 1 - place])
    return blocks.transpose(*turned, *range(len(order), blocks.ndim)).reshape(-1, *shard.shape)


def gather_axes(shard, axes, order, dim):
    return joined_along(all_blocks(shard, axes, order), dim)


def cut_along(shard, dim, count):
    before, after = (shard.shape[:dim], shard.shape[dim + 1 :])
    return jnp.moveaxis(shard.reshape(*before, count, -1, *after), dim, 0)


def sent_and_summed(shard, axis, dim):
    count = lax.axis_size(axis)
    blocks = lax.all_to_all(cut_along(shard, dim, count), axis, 0, 0, tiled=True)
    return jnp.sum(blocks.astype(jnp.float32), axis=0)


def of_everyone(shard, axis):
    everything = from_everyone(shard, axis)
    return jnp.sum(everything, axis=0)


def rotate(values, position, width):
    count = values.shape[1] // width
    half = width // 2
    shaped = values.reshape(values.shape[0], count, width)
    freq = 10000.0 ** (-(jnp.arange(half, dtype=jnp.float32) / half))
    angle = position[:, None] * freq[None, :]
    cosine = jnp.cos(angle)[:, None, :]
    sine = jnp.sin(angle)[:, None, :]
    first = shaped[:, :, :half]
    second = shaped[:, :, half:]
    turned = jnp.concatenate(
        [first * cosine - second * sine, second * cosine + first * sine], axis=2
    )
    return turned.reshape(values.shape[0], count * width)


def add_counts(earlier, later):
    return earlier + later


def local(tokens, segments, pre_gain, post_gain, w_query, w_key, w_value, w_out):
    rows = tokens.shape[0]
    whole = lax.all_gather(tokens, "head", axis=1, tiled=True)
    wide = whole.astype(jnp.float32)
    normed = (
        wide * lax.rsqrt(jnp.mean(wide * wide, axis=1, keepdims=True) + EPS) * pre_gain
    ).astype(jnp.bfloat16)
    pieces = sent_together((w_query, w_key, w_value), SEQ, 0, 1)
    query, key_proj, value_proj = tuple(
        (jnp.dot(normed, piece, preferred_element_type=jnp.float32) for piece in pieces)
    )
    levels = jnp.arange(DOCS, dtype=jnp.int32)
    below = jnp.sum((levels[None, :] > segments[:, None]).astype(jnp.float32), axis=0)
    earlier = entering(below, SEQ, add_counts, jnp.zeros((DOCS,), jnp.float32))
    starts = earlier + below
    onehot = (segments[:, None] == levels[None, :]).astype(jnp.float32)
    tok_start = jnp.sum(onehot * starts[None, :], axis=1)
    offset = lax.axis_index(SEQ) * rows
    index_f = (offset + jnp.arange(rows, dtype=jnp.int32)).astype(jnp.float32)
    position = index_f - tok_start
    kv_count = w_key.shape[1] // HD
    rq = (rotate(query, position, HD) * SCALAR ** (-0.5)).astype(jnp.bfloat16)
    rk = rotate(key_proj, position, HD).astype(jnp.bfloat16)
    vb = value_proj.astype(jnp.bfloat16)
    stacked = (
        rq.reshape(rows, kv_count, GROUP, HD)
        .transpose(1, 2, 0, 3)
        .reshape(kv_count, GROUP * rows, HD)
    )
    query_start = jnp.tile(tok_start, GROUP)
    query_index = jnp.tile(index_f, GROUP)
    first_start = tok_start[0]
    last_index = index_f[rows - 1]
    empty = (
        jnp.zeros((kv_count, GROUP * rows, HD), jnp.float32),
        jnp.zeros((kv_count, GROUP * rows), jnp.float32),
    )
    keys_all, values_all = sent_together((rk, vb), SEQ, 0, 1)
    count = keys_all.shape[0]
    block = 1024
    steps_total = count // block

    def compute(offset_blk, state):
        numer, denom = state
        keys_blk = lax.dynamic_slice_in_dim(keys_all, offset_blk, block, 0).reshape(
            block, kv_count, HD
        )
        values_blk = lax.dynamic_slice_in_dim(values_all, offset_blk, block, 0).reshape(
            block, kv_count, HD
        )
        key_index = (offset_blk + jnp.arange(block, dtype=jnp.int32)).astype(jnp.float32)
        scores = jnp.einsum("cqd,kcd->cqk", stacked, keys_blk, preferred_element_type=jnp.float32)
        capped = CAP * jnp.tanh(scores / CAP)
        allowed = (key_index[None, None, :] >= query_start[None, :, None]) & (
            key_index[None, None, :] <= query_index[None, :, None]
        )
        weights = jnp.where(allowed, jnp.exp(capped), 0.0)
        numer = numer + jnp.einsum(
            "cqk,kcd->cqd",
            weights.astype(jnp.bfloat16),
            values_blk,
            preferred_element_type=jnp.float32,
        )
        denom = denom + jnp.sum(weights, axis=2)
        return (numer, denom)

    def one_block(step, state):
        offset_blk = step * block
        first_key = offset_blk.astype(jnp.float32)
        live = (first_key <= last_index) & (first_key + (block - 1) >= first_start)
        return lax.cond(live, lambda s: compute(offset_blk, s), lambda s: s, state)

    numer, denom = lax.fori_loop(0, steps_total, one_block, empty)
    attn = (numer / denom[:, :, None]).reshape(kv_count, GROUP, rows, HD).transpose(2, 0, 1, 3)
    attn = attn.reshape(rows, kv_count * GROUP * HD).astype(jnp.bfloat16)
    partial_proj = jnp.dot(
        attn, gather_axes(w_out, SEQ, (0, 1), 1), preferred_element_type=jnp.float32
    )
    partial_proj = lax.optimization_barrier(partial_proj.astype(jnp.bfloat16)).astype(jnp.float32)
    share = sent_and_summed(partial_proj.astype(jnp.bfloat16), "head", 1)
    squares = of_everyone(jnp.sum(share * share, axis=1), "head")
    width = share.shape[1]
    gain_part = lax.dynamic_slice_in_dim(post_gain, lax.axis_index("head") * width, width)
    scale = lax.rsqrt(squares[:, None] / D + EPS)
    own = tokens.astype(jnp.float32)
    result = (own + share * scale * gain_part).astype(jnp.bfloat16)
    return lax.all_gather(result, "head", axis=1, tiled=True)


def solution(mesh):
    finer = Mesh(mesh.devices.reshape(2, 16, mesh.shape["head"]), ("seq_0", "seq_1", "head"))
    in_specs = (
        P(SEQ, "head"),
        P(SEQ),
        P(),
        P(),
        P(SEQ, "head"),
        P(SEQ, "head"),
        P(SEQ, "head"),
        P("head", SEQ),
    )
    out_specs = P(SEQ, None)
    return jax.shard_map(local, mesh=finer, in_specs=in_specs, out_specs=out_specs, check_vma=False)
```

profile of v0, /device:TPU:1, one launch (start us, length us, event | category | flops | bytes accessed | tf_op | source)
XLA Modules:
  0.0 593.6 jit_solution(15508879731731591782)
XLA Ops:
  6.5 0.0 copy-start.3
  6.5 0.0 all-gather.7.cloned.1.call-start
  6.5 0.7 all-gather.7.cloned.1.call-update
  7.3 0.0 all-gather.9.cloned.1.call-start
  7.3 1.6 pad_maximum_fusion
  8.9 0.0 all-gather.9.cloned.1.call-update
  8.9 0.0 all-gather.13.cloned.1.call-start
  9.0 6.2 %all-gather = bf16[512,144]{0,1:T(8,128)(2,1)S(1)} all-gather(bf16[256,144]{0,1:T(8,128)(2,1)} %param.19), channel_id=2, replica_groups=mesh['seq_0'=2,'seq_1'=16,'head'=16] {'seq_0'}, dimensions={0}, use_global_device_ids=true | all-gather | bytes 221184 | tf_op jit(solution)/shard_map/all_gather | solution.py:60
  15.2 0.7 copy.63
  15.9 0.0 all-gather.13.cloned.1.call-update
  15.9 0.8 convert_reduce_fusion.1
  16.7 0.6 broadcast_in_dim.28
  17.3 17.8 %all-to-all-start = ((f32[32,1,8]{2,1,0:T(1,128)}), f32[32,1,8]{2,1,0:T(1,128)S(1)}, u32[]{:S(2)}, u32[]{:S(2)}) async-start(f32[32,1,8]{2,1,0:T(1,128)} %broadcast_in_dim.28), calls=%async_computation | async-start | bytes 32768 | tf_op jit(solution)/shard_map/all_to_all | solution.py:28
  35.1 0.0 all-gather.11.cloned.1.call-start
  35.2 13.6 %all-to-all-done = f32[32,1,8]{2,1,0:T(1,128)S(1)} async-done(((f32[32,1,8]{2,1,0:T(1,128)}), f32[32,1,8]{2,1,0:T(1,128)S(1)}, u32[]{:S(2)}, u32[]{:S(2)}) %all-to-all-start) | async-done | bytes 1056 | tf_op jit(solution)/shard_map/all_to_all | solution.py:28
  48.8 0.1 broadcast_select_fusion
  49.1 0.8 select_reduce_fusion
  49.9 7.3 %all-gather.7.cloned.1.call-done = bf16[256,4608]{0,1:T(8,128)(2,1)} async-done(((bf16[256,288]{0,1:T(8,128)(2,1)}), bf16[256,4608]{0,1:T(8,128)(2,1)}) %all-gather.7.cloned.1.call-update) | async-done | bytes 2359312 | tf_op jit(solution)/shard_map/all_gather | solution.py:109
  57.2 0.0 copy-start
  57.2 2.5 fusion.11
  59.7 158.6 %all-gather.9.cloned.1.call-done = bf16[4608,512]{1,0:T(8,128)(2,1)} async-done(((bf16[144,512]{1,0:T(8,128)(2,1)}), bf16[4608,512]{1,0:T(8,128)(2,1)}) %all-gather.9.cloned.1.call-update) | async-done | bytes 4718608 | tf_op jit(solution)/shard_map/all_gather | solution.py:22
  218.3 0.0 copy-done.3
  218.3 0.0 copy-done
  218.3 2.5 fusion.20
  220.8 0.3 fusion.33
  221.2 2.5 fusion.23
  223.6 0.7 pad_maximum_fusion.1
  224.3 0.0 all-gather.11.cloned.1.call-update
  224.3 0.6 slice.50
  224.9 0.6 slice.61
  225.5 0.3 multiply_cosine_fusion
  225.8 61.7 %all-gather.13.cloned.1.call-done = bf16[32,256,144]{1,2,0:T(8,128)(2,1)} async-done(((bf16[2,256,144]{1,2,0:T(8,128)(2,1)}), bf16[32,256,144]{1,2,0:T(8,128)(2,1)}) %all-gather.13.cloned.1.call-update) | async-done | bytes 2359312 | tf_op jit(solution)/shard_map/all_gather | solution.py:60
  287.5 0.0 copy-start.1
  287.5 2.0 copy.54
  289.5 0.4 copy-done.1
  289.9 3.2 fusion.14
  293.2 0.1 copy.49
  293.3 158.9 %all-gather.11.cloned.1.call-done = bf16[8192,256]{0,1:T(8,128)(2,1)} async-done(((bf16[256,256]{0,1:T(8,128)(2,1)}), bf16[8192,256]{0,1:T(8,128)(2,1)}) %all-gather.11.cloned.1.call-update) | async-done | bytes 4194320 | tf_op jit(solution)/shard_map/all_gather | solution.py:22
  452.3 4.7 fusion.42
  456.9 4.1 copy.51
  461.0 4.1 copy.50
  465.1 13.7 %while.16 = (s32[]{:T(128)}, f32[1,512,128]{2,1,0:T(8,128)S(1)}, f32[1,512]{1,0:T(1,128)S(1)}, f32[]{:T(128)}, f32[]{:T(128)}, /*index=5*/bf16[8192,128]{1,0:T(8...) while((s32[]{:T(128)}, f32[1,512,128]{2,1,0:T(8,128)S(1)}, ...), condition=%wide.region_7.8_spmd.clone, body=%wide.region_3.7_spmd.clone.sunk | while | flops 272697344 | bytes 3311949 | solution.py:179
  466.4 3.4 conditional.3
  466.4 1.9 fusion.41
  468.3 1.4 fusion.4
  478.8 0.1 divide_convert_fusion
  479.0 0.1 copy.52
  479.1 2.2 convolution_convert_fusion
  481.3 2.8 copy.55
  484.2 44.6 %all_to_all.20 = bf16[16,256,288]{1,2,0:T(8,128)(2,1)S(1)} all-to-all(bf16[16,256,288]{1,2,0:T(8,128)(2,1)S(1)} %bitcast.63), channel_id=1, replica_groups=mesh['seq_0'=2,'seq_1'=16,'head'=16] {'head'}, dimensions={0} | all-to-all | bytes 4718592 | tf_op jit(solution)/shard_map/all_to_all | solution.py:78
  528.8 0.0 copy-start.2
  528.8 0.3 convert_reduce_fusion
  529.1 0.1 multiply_reduce_fusion
  529.2 0.6 broadcast_in_dim.34
  529.8 4.2 all-to-all-start.2
  534.0 0.0 all-gather.15.cloned.1.call-start
  534.1 0.8 dynamic_slice.9
  534.8 5.0 all-to-all-done.2
  539.9 0.0 copy-done.2
  539.9 0.8 add_convert_fusion.1
  540.7 0.0 all-gather.15.cloned.1.call-update
  540.7 42.1 %all-gather.15.cloned.1.call-done = bf16[256,4608]{0,1:T(8,128)(2,1)} async-done(((bf16[256,288]{0,1:T(8,128)(2,1)}), bf16[256,4608]{0,1:T(8,128)(2,1)}) %all-gather.15.cloned.1.call-update) | async-done | bytes 2359312 | tf_op jit(solution)/shard_map/all_gather | solution.py:193
  582.8 4.3 copy.57
  (37 shorter events, 0.5 us)
Async XLA Ops:
  6.5 211.8 %copy-start.3 = (f32[4608]{0:T(1024)S(1)}, f32[4608]{0:T(1024)}, u32[]{:S(2)}) copy-start(f32[4608]{0:T(1024)} %param.14) | copy-start | bytes 55300
  6.5 50.7 %all-gather.7.cloned.1.call-start = ((), (), s32[]{:S(2)}) async-start(), calls=%async_computation.3 | async-start | bytes 2506752 | tf_op jit(solution)/shard_map/all_gather | solution.py:109
  7.3 211.1 %all-gather.9.cloned.1.call-start = ((), (), s32[]{:S(2)}) async-start(), calls=%async_computation.4 | async-start | bytes 4866048 | tf_op jit(solution)/shard_map/all_gather | solution.py:22
  8.9 278.6 %all-gather.13.cloned.1.call-start = ((), (), s32[]{:S(2)}) async-start(), calls=%async_computation.6 | async-start | bytes 2506752 | tf_op jit(solution)/shard_map/all_gather | solution.py:60
  17.3 31.5 %all-to-all-start = ((f32[32,1,8]{2,1,0:T(1,128)}), f32[32,1,8]{2,1,0:T(1,128)S(1)}, u32[]{:S(2)}, u32[]{:S(2)}) async-start(f32[32,1,8]{2,1,0:T(1,128)} %broadcast_in_dim.28), calls=%async_computation | async-start | bytes 32768 | tf_op jit(solution)/shard_map/all_to_all | solution.py:28
  35.1 417.1 %all-gather.11.cloned.1.call-start = ((), (), s32[]{:S(2)}) async-start(), calls=%async_computation.5 | async-start | bytes 4325376 | tf_op jit(solution)/shard_map/all_gather | solution.py:22
  57.2 161.1 %copy-start = (bf16[256,4608]{0,1:T(8,128)(2,1)S(1)}, bf16[256,4608]{0,1:T(8,128)(2,1)}, u32[]{:S(2)}) copy-start(bf16[256,4608]{0,1:T(8,128)(2,1)} %all-gather.7.cloned.1.call-done) | copy-start | bytes 7077892
  287.5 2.4 copy-start.1
  528.8 11.1 %copy-start.2 = (bf16[256,288]{0,1:T(8,128)(2,1)S(1)}, bf16[256,288]{0,1:T(8,128)(2,1)}, u32[]{:S(2)}) copy-start(bf16[256,288]{0,1:T(8,128)(2,1)} %param.12) | copy-start | bytes 442372
  529.8 10.1 %all-to-all-start.2 = ((f32[16,1,256]{2,1,0:T(1,128)}), f32[16,1,256]{2,1,0:T(1,128)S(1)}, u32[]{:S(2)}, u32[]{:S(2)}) async-start(f32[16,1,256]{2,1,0:T(1,128)} %broadcast_in_dim.34), calls=%async_computation.2 | async-start | bytes 32768 | tf_op jit(solution)/shard_map/all_to_all | solution.py:28
  534.0 48.8 %all-gather.15.cloned.1.call-start = ((), (), s32[]{:S(2)}) async-start(), calls=%async_computation.7 | async-start | bytes 2506752 | tf_op jit(solution)/shard_map/all_gather | solution.py:193
Sparse Core Ops, SparseCore 0:
  9.5 47.6 all-gather.6
  60.3 157.9 all-gather.8
  220.4 67.0 all-gather.12
  290.3 161.9 all-gather.10
  540.8 41.9 all-gather.14
where the time goes:
time: 598 us; the launch traced here: 594 us
  waiting for transfers between devices  448 us (75%)
  blocking collectives  50.9 us (9%)
  local copies, waits for them, and re-layouts  26.5 us (4%)
  starting transfers between devices  22.2 us (4%)
  matrix products  13.7 us (2%)
  between operations  13.3 us (2%)
  loops' own time  10.4 us (2%)
  other arithmetic  8.47 us (1%)
    all_gather x2, waiting for transfers between devices, sent_together(): filled = lax.all_gather(both, axis, axis=dim, tiled=True)  318 us
    all_gather x1, waiting for transfers between devices, all_blocks(): blocks = lax.all_gather(blocks, axes[k], axis=0, tiled=True)  61.7 us
    all_to_all x1, blocking collectives, sent_and_summed(): lax.all_to_all(cut_along(shard, dim, count), axis, 0, 0, tiled=True)  44.6 us
    all_gather x1, waiting for transfers between devices, local(): return lax.all_gather(result, 'head', axis=1, tiled=True)  42.1 us
    all_to_all x2, starting transfers between devices, from_everyone(): return lax.all_to_all(copies, axis, split_axis=0, concat_axis=0, tiled=True)  22 us
    all_to_all x2, waiting for transfers between devices, from_everyone(): return lax.all_to_all(copies, axis, split_axis=0, concat_axis=0, tiled=True)  18.6 us
  transfers between devices with their start and end apart: 7, of which 7 were waited for; matrix products, arithmetic and copies ran while one was open for 3% of the time, Pallas kernels for 0%

commit v1 on v0

v1 whole, which is shorter than its diff:
```python
import jax
import jax.numpy as jnp
from jax import lax
from jax.experimental import pallas as pl
from jax.experimental.pallas import tpu as pltpu
from jax.sharding import Mesh
from jax.sharding import PartitionSpec as P

D = 4608
HD = 128
GROUP = 2
SCALAR = 144
DOCS = 8
SEQ = ("xh", "z")
HEAD = ("xl", "y", "c")
PLANE = ("xl", "y")

EPS = 1e-06
CAP = 50.0


def from_everyone(shard, axis):
    copies = jnp.broadcast_to(shard, (lax.axis_size(axis), *shard.shape))
    return lax.all_to_all(copies, axis, split_axis=0, concat_axis=0, tiled=True)


def rotate(values, cosine, sine):
    half = values.shape[1] // 2
    first = values[:, :half]
    second = values[:, half:]
    return jnp.concatenate(
        [first * cosine - second * sine, second * cosine + first * sine], axis=1
    )


def attend_kernel(where_ref, query_ref, start_ref, kv_hbm, out_ref, held, sums, total, sem):
    rows = query_ref.shape[0] // GROUP
    low = where_ref[0]
    own = where_ref[1]
    halves = where_ref[2]

    def fetch(j):
        place = (lax.rem(j, halves) * 2 + lax.div(j, halves)) * rows
        return pltpu.make_async_copy(
            kv_hbm.at[pl.ds(pl.multiple_of(place, rows), rows), :], held.at[j], sem.at[j]
        )

    @pl.loop(low, own + 1)
    def _(j):
        fetch(j).start()

    sums[...] = jnp.zeros_like(sums)
    total[...] = jnp.zeros_like(total)
    shape = (GROUP * rows, rows)
    row = lax.broadcasted_iota(jnp.int32, shape, 0)
    index = own * rows + jnp.where(row >= rows, row - rows, row)
    column = lax.broadcasted_iota(jnp.int32, shape, 1)

    @pl.loop(low, own + 1)
    def _(j):
        fetch(j).wait()
        keys = held[j, :, :HD]
        values = held[j, :, HD:]
        scores = lax.dot_general(
            query_ref[...], keys, (((1,), (1,)), ((), ())), preferred_element_type=jnp.float32
        )
        weights = jnp.exp(CAP * jnp.tanh(scores * (1.0 / CAP)))
        key_index = j * rows + column
        allowed = (key_index >= start_ref[...]) & (key_index <= index)
        weights = jnp.where(allowed, weights, 0.0)
        part = weights[:, :HD]
        for k in range(1, rows // HD):
            part = part + weights[:, k * HD : (k + 1) * HD]
        sums[...] += part
        total[...] += jnp.dot(
            weights.astype(jnp.bfloat16), values, preferred_element_type=jnp.float32
        )

    result = total[...] / jnp.sum(sums[...], axis=1, keepdims=True)
    for k in range(GROUP):
        out_ref[:, k * HD : (k + 1) * HD] = result[k * rows : (k + 1) * rows].astype(jnp.bfloat16)


def attend(where, stacked, starts, kv):
    rows = stacked.shape[0] // GROUP
    blocks = kv.shape[0] // rows
    vmem = pl.BlockSpec(memory_space=pltpu.VMEM)
    return pl.pallas_call(
        attend_kernel,
        out_shape=jax.ShapeDtypeStruct((rows, GROUP * HD), jnp.bfloat16),
        in_specs=[
            pl.BlockSpec(memory_space=pltpu.SMEM),
            vmem,
            vmem,
            pl.BlockSpec(memory_space=pl.ANY),
        ],
        out_specs=vmem,
        scratch_shapes=[
            pltpu.VMEM((blocks, rows, 2 * HD), jnp.bfloat16),
            pltpu.VMEM((GROUP * rows, HD), jnp.float32),
            pltpu.VMEM((GROUP * rows, HD), jnp.float32),
            pltpu.SemaphoreType.DMA((blocks,)),
        ],
        compiler_params=pltpu.CompilerParams(vmem_limit_bytes=24 * 1024 * 1024),
        cost_estimate=pl.CostEstimate(
            flops=4 * GROUP * rows * HD * kv.shape[0] // 2,
            bytes_accessed=kv.size,
            transcendentals=GROUP * rows * kv.shape[0],
        ),
    )(where, stacked, starts, kv)


def local(tokens, segments, pre_gain, post_gain, w_query, w_key, w_value, w_out):
    rows = tokens.shape[0]
    deep = lax.axis_size("z")
    slab = w_key.shape[0]
    mine = jnp.concatenate([w_key, w_value, w_query, w_out.T], axis=1)
    pair = lax.all_gather(mine, "xh", axis=0, tiled=True)
    weights = lax.all_gather(pair, "z", axis=0, tiled=True)

    whole = from_everyone(tokens.T, HEAD).reshape(D, rows)
    wide = whole.astype(jnp.float32)
    scale = lax.rsqrt(jnp.mean(wide * wide, axis=0, keepdims=True) + EPS)
    normed = (wide * scale * pre_gain[:, None]).astype(jnp.bfloat16)
    normed = normed.reshape(2, deep, slab, rows).transpose(1, 0, 2, 3).reshape(D, rows).T
    normed = lax.optimization_barrier(normed)

    levels = jnp.arange(DOCS, dtype=jnp.int32)
    counts = jnp.sum((levels[None, :] > segments[:, None]).astype(jnp.float32), axis=0)
    starts = jnp.sum(from_everyone(counts, SEQ).reshape(-1, DOCS), axis=0)
    onehot = (segments[:, None] == levels[None, :]).astype(jnp.float32)
    tok_start = jnp.sum(onehot * starts[None, :], axis=1)
    block = lax.axis_index(SEQ)
    index_f = (block * rows + jnp.arange(rows, dtype=jnp.int32)).astype(jnp.float32)
    position = index_f - tok_start
    half = HD // 2
    freq = 10000.0 ** (-(jnp.arange(half, dtype=jnp.float32) / half))
    angle = position[:, None] * freq[None, :]
    cosine, sine = jnp.cos(angle), jnp.sin(angle)
    start_i = tok_start.astype(jnp.int32)
    where = jnp.stack([start_i[0] // rows, block.astype(jnp.int32), jnp.int32(deep)])
    starts_col = jnp.tile(start_i, GROUP)[:, None]

    kv = jnp.dot(normed, weights[:, : 2 * HD], preferred_element_type=jnp.float32)
    rk = rotate(kv[:, :HD], cosine, sine).astype(jnp.bfloat16)
    vb = kv[:, HD:].astype(jnp.bfloat16)
    kv_pair = lax.all_gather(jnp.concatenate([rk, vb], axis=1), "xh", axis=0, tiled=True)
    kv_all = lax.all_gather(kv_pair, "z", axis=0, tiled=True)

    query = jnp.dot(normed, weights[:, 2 * HD : 4 * HD], preferred_element_type=jnp.float32)
    stacked = jnp.concatenate(
        [
            (rotate(query[:, k * HD : (k + 1) * HD], cosine, sine) * SCALAR ** (-0.5)).astype(
                jnp.bfloat16
            )
            for k in range(GROUP)
        ],
        axis=0,
    )
    out_t = weights[:, 4 * HD :].reshape(deep, 2, slab, GROUP * HD).transpose(1, 0, 2, 3)
    out_t = lax.optimization_barrier(out_t.reshape(D, GROUP * HD))

    near = lax.axis_size(PLANE)
    few = rows // (near * lax.axis_size("c"))
    first_row = (lax.axis_index("c") * near + lax.axis_index(PLANE)) * few
    own = lax.dynamic_slice_in_dim(whole, first_row, few, 1).T.astype(jnp.float32)

    attn = attend(where, stacked, starts_col, kv_all)
    partial = lax.dot_general(
        attn, out_t, (((1,), (1,)), ((), ())), preferred_element_type=jnp.float32
    ).astype(jnp.bfloat16)

    halves = lax.all_to_all(partial.reshape(2, rows // 2, D), "c", 0, 0, tiled=True)
    halves = (halves[0].astype(jnp.float32) + halves[1].astype(jnp.float32)).astype(jnp.bfloat16)
    pieces = lax.all_to_all(halves.reshape(near, few, D), PLANE, 0, 0, tiled=True)
    proj = jnp.sum(pieces.astype(jnp.float32), axis=0)
    post = lax.rsqrt(jnp.mean(proj * proj, axis=1, keepdims=True) + EPS)
    result = (own + proj * post * post_gain[None, :]).astype(jnp.bfloat16)
    result = from_everyone(result, PLANE).reshape(rows // 2, D)
    return from_everyone(result, "c").reshape(rows, D)


def solution(mesh):
    finer = Mesh(mesh.devices.reshape(2, 16, 2, 4, 2), ("xh", "z", "xl", "y", "c"))
    in_specs = (
        P(SEQ, HEAD),
        P(SEQ),
        P(),
        P(),
        P(SEQ, HEAD),
        P(SEQ, HEAD),
        P(SEQ, HEAD),
        P(HEAD, SEQ),
    )
    return jax.shard_map(
        local, mesh=finer, in_specs=in_specs, out_specs=P(SEQ, None), check_vma=False
    )
```

time: 598 us -> 281 us (0.47)
  the two profiles are of different devices: /device:TPU:1 before, /device:TPU:37 now
where the time goes in v1:
time: 281 us
  waiting for transfers between devices  130 us (46%)
  blocking collectives  84.6 us (30%)
  between operations  16.2 us (6%)
  local copies, waits for them, and re-layouts  16.1 us (6%)
  starting transfers between devices  12.9 us (5%)
  Pallas kernels  9.42 us (3%)
  matrix products  6.62 us (2%)
  other arithmetic  5.99 us (2%)
    all_gather x1, waiting for transfers between devices, local(): kv_all = lax.all_gather(kv_pair, 'z', axis=0, tiled=True)  62.6 us
    all_to_all x3, blocking collectives, from_everyone(): return lax.all_to_all(copies, axis, split_axis=0, concat_axis=0, tiled=True)  54.2 us
    all_to_all x1, waiting for transfers between devices, from_everyone(): return lax.all_to_all(copies, axis, split_axis=0, concat_axis=0, tiled=True)  30.3 us
    all_gather x1, waiting for transfers between devices, local(): weights = lax.all_gather(pair, 'z', axis=0, tiled=True)  23.4 us
    all_to_all x1, blocking collectives, local(): lax.all_to_all(partial.reshape(2, rows // 2, D), 'c', 0, 0, tiled=True)  15.7 us
    all_to_all x1, waiting for transfers between devices, local(): lax.all_to_all(halves.reshape(near, few, D), PLANE, 0, 0, tiled=True)  13.3 us
    pallas_call x1, Pallas kernels, attend(): pl.pallas_call(attend_kernel, out_shape=jax.ShapeDtypeStruct((rows, GROUP...  9.42 us
    all_gather x1, blocking collectives, local(): pair = lax.all_gather(mine, 'xh', axis=0, tiled=True)  8.58 us
  transfers between devices with their start and end apart: 4, of which 4 were waited for; matrix products, arithmetic and copies ran while one was open for 4% of the time, Pallas kernels for 0%

profile of v1, /device:TPU:37, one launch (start us, length us, event | category | flops | bytes accessed | tf_op | source)
XLA Modules:
  0.0 281.4 jit_solution(10598845508157333202)
XLA Ops:
  6.5 0.0 all-gather.3.cloned.1.call-start
  6.5 0.9 pad_maximum_fusion
  7.5 8.6 %all_gather.12 = bf16[288,768]{1,0:T(8,128)(2,1)} all-gather(bf16[144,768]{1,0:T(8,128)(2,1)S(1)} %pad_maximum_fusion), channel_id=1, replica_groups=mesh['xh'=2,'z'=16,'xl'=2,'y'=4,'c'=2] {'xh'}, dimensions={0}, use_global_device_ids=true | all-gather | bytes 663552 | tf_op jit(solution)/shard_map/all_gather | solution.py:118
  16.1 0.0 all-gather.3.cloned.1.call-update
  16.1 0.8 convert_reduce_fusion.1
  16.9 27.4 %all_to_all.31 = f32[32,1,8]{2,1,0:T(1,128)S(1)} all-to-all(f32[32,1,8]{2,1,0:T(1,128)S(1)} %broadcast_in_dim.9), channel_id=1, replica_groups=mesh['xh'=2,'z'=16,'xl'=2,'y'=4,'c'=2] {'xh','z'}, dimensions={0} | all-to-all | bytes 2048 | tf_op jit(solution)/shard_map/all_to_all | solution.py:24
  44.3 2.5 broadcast_in_dim.8
  46.8 0.0 copy-start.4
  46.8 0.0 copy-start.5
  46.8 8.3 %all-to-all-start = ((bf16[16,288,256]{2,1,0:T(8,128)(2,1)}), bf16[16,288,256]{2,1,0:T(8,128)(2,1)S(1)}, u32[]{:S(2)}, u32[]{:S(2)}) async-start(bf16[16,288,256]{2,1,0:T(8,128)(2,1)} %broadcast_in_dim.8), calls=%async_computation | async-start | bytes 4718592 | tf_op jit(solution)/shard_map/all_to_all | solution.py:24
  55.1 0.0 all-gather.5.cloned.1.call-start
  55.1 0.0 copy-done.4
  55.1 0.1 mul.130
  55.2 0.1 reduce_sum.55
  55.3 0.0 copy-done.5
  55.3 0.1 select_reduce_fusion
  55.4 30.3 %all-to-all-done = bf16[16,288,256]{2,1,0:T(8,128)(2,1)S(1)} async-done(((bf16[16,288,256]{2,1,0:T(8,128)(2,1)}), bf16[16,288,256]{2,1,0:T(8,128)(2,1)S(1)}, u32[]{:S(2)}, u32[]{:S(2)}) %all-to-all-start) | async-done | bytes 2359328 | tf_op jit(solution)/shard_map/all_to_all | solution.py:24
  85.6 0.6 multiply_reduce_fusion
  86.3 0.8 fusion
  87.1 1.6 copy.62
  88.7 23.4 %all-gather.3.cloned.1.call-done = bf16[4608,768]{1,0:T(8,128)(2,1)} async-done(((bf16[288,768]{1,0:T(8,128)(2,1)}), bf16[4608,768]{1,0:T(8,128)(2,1)}) %all-gather.3.cloned.1.call-update) | async-done | bytes 7077904 | tf_op jit(solution)/shard_map/all_gather | solution.py:119
  112.1 0.0 copy-start.2
  112.1 3.3 %fusion.1 = f32[256,256]{1,0:T(8,128)S(1)} fusion(bf16[256,4608]{0,1:T(8,128)(2,1)} %bitcast.42, bf16[4608,768]{1,0:T(8,128)(2,1)} %all-gather.3.cloned.1.call-done), kind=kOutput, calls=%fused_computation.4 | convolution fusion | flops 603979776 | bytes 4980736 | tf_op jit(solution)/shard_map/dot_general | solution.py:144
  115.5 1.1 copy-done.2
  116.6 2.5 fusion.3
  119.1 0.6 fusion.23
  119.7 0.1 pad_maximum_fusion.2
  119.8 6.1 %all_gather.14 = bf16[512,256]{1,0:T(8,128)(2,1)} all-gather(bf16[256,256]{1,0:T(8,128)(2,1)S(1)} %pad_maximum_fusion.2), channel_id=1, replica_groups=mesh['xh'=2,'z'=16,'xl'=2,'y'=4,'c'=2] {'xh'}, dimensions={0}, use_global_device_ids=true | all-gather | bytes 393216 | tf_op jit(solution)/shard_map/all_gather | solution.py:147
  125.9 0.0 all-gather.5.cloned.1.call-update
  125.9 0.5 slice.49
  129.1 0.1 copy.77
  129.2 0.1 pad_add_fusion.where_ref
  129.3 0.0 slice-start
  129.3 1.7 slice-done
  131.0 1.6 copy.71
  132.5 0.1 fusion.26
  132.7 62.6 %all-gather.5.cloned.1.call-done.kv_hbm = bf16[8192,256]{1,0:T(8,128)(2,1)} async-done(((bf16[512,256]{1,0:T(8,128)(2,1)}), bf16[8192,256]{1,0:T(8,128)(2,1)}) %all-gather.5.cloned.1.call-update) | async-done | bytes 4194320 | tf_op jit(solution)/shard_map/all_gather | solution.py:148
  195.2 0.0 copy-start
  195.2 2.2 copy-done
  197.4 0.0 copy-start.1
  197.4 9.4 %shard_map.82 = bf16[256,256]{1,0:T(8,128)(2,1)S(1)} custom-call(s32[3]{0:T(128)S(1)} %pad_add_fusion.where_ref, bf16[512,128]{1,0:T(8,128)(2,1)S(1)} %pad_maximum_fusion.1.query_ref, s32[512,1]{1,0:T(8,128)S(1)} %bitcast.34, bf16[8192,256]{1,0:T(8,128)(2,1)S(1)} %copy-done), custom_call_target="tpu_custom_call" | custom-call | flops 1073741824 | bytes 2097152 | tf_op jit(solution)/shard_map/pallas_call | solution.py:88
  206.9 0.0 copy-done.1
  206.9 0.8 convolution_convert_fusion
  207.7 15.7 %all_to_all.32 = bf16[2,128,4608]{2,1,0:T(8,128)(2,1)S(1)} all-to-all(bf16[2,128,4608]{2,1,0:T(8,128)(2,1)S(1)} %bitcast.38), channel_id=1, replica_groups=mesh['xh'=2,'z'=16,'xl'=2,'y'=4,'c'=2] {'c'}, dimensions={0} | all-to-all | bytes 4718592 | tf_op jit(solution)/shard_map/all_to_all | solution.py:173
  223.4 1.3 add_convert_fusion
  224.6 4.6 %all-to-all-start.3 = ((bf16[8,16,4608]{2,1,0:T(8,128)(2,1)}), bf16[8,16,4608]{2,1,0:T(8,128)(2,1)S(1)}, u32[]{:S(2)}, u32[]{:S(2)}) async-start(bf16[8,16,4608]{2,1,0:T(8,128)(2,1)} %bitcast.15), calls=%async_computation.3 | async-start | bytes 2359296 | tf_op jit(solution)/shard_map/all_to_all | solution.py:175
  229.3 1.4 constant_dynamic-slice_fusion
  230.7 0.0 copy-start.3
  230.7 1.6 copy.75
  232.3 13.3 %all-to-all-done.3 = bf16[8,16,4608]{2,1,0:T(8,128)(2,1)S(1)} async-done(((bf16[8,16,4608]{2,1,0:T(8,128)(2,1)}), bf16[8,16,4608]{2,1,0:T(8,128)(2,1)S(1)}, u32[]{:S(2)}, u32[]{:S(2)}) %all-to-all-start.3) | async-done | bytes 1179680 | tf_op jit(solution)/shard_map/all_to_all | solution.py:175
  245.6 0.2 convert_reduce_fusion
  245.8 0.2 multiply_reduce_fusion.1
  246.0 0.0 copy-done.3
  246.0 0.1 fusion.5
  246.1 0.1 broadcast_in_dim.10
  246.2 19.6 %all_to_all.33 = bf16[8,16,4608]{2,1,0:T(8,128)(2,1)S(1)} all-to-all(bf16[8,16,4608]{2,1,0:T(8,128)(2,1)S(1)} %broadcast_in_dim.10), channel_id=1, replica_groups=mesh['xh'=2,'z'=16,'xl'=2,'y'=4,'c'=2] {'xl','y'}, dimensions={0} | all-to-all | bytes 2359296 | tf_op jit(solution)/shard_map/all_to_all | solution.py:24
  265.8 0.2 broadcast_in_dim.11
  265.9 7.2 %all_to_all.34 = bf16[2,128,4608]{2,1,0:T(8,128)(2,1)S(1)} all-to-all(bf16[2,128,4608]{2,1,0:T(8,128)(2,1)S(1)} %broadcast_in_dim.11), channel_id=1, replica_groups=mesh['xh'=2,'z'=16,'xl'=2,'y'=4,'c'=2] {'c'}, dimensions={0} | all-to-all | bytes 4718592 | tf_op jit(solution)/shard_map/all_to_all | solution.py:24
  273.2 1.4 copy.79
  (9 shorter events, 0.1 us)
Async XLA Ops:
  6.5 105.6 %all-gather.3.cloned.1.call-start = ((), (), s32[]{:S(2)}) async-start(), calls=%async_computation.6 | async-start | bytes 7520256 | tf_op jit(solution)/shard_map/all_gather | solution.py:119
  46.8 8.3 %copy-start.4 = (f32[4608]{0:T(1024)S(1)}, f32[4608]{0:T(1024)}, u32[]{:S(2)}) copy-start(f32[4608]{0:T(1024)} %param.10) | copy-start | bytes 55300
  46.8 8.5 %copy-start.5 = (s32[256]{0:T(256)S(1)}, s32[256]{0:T(256)}, u32[]{:S(2)}) copy-start(s32[256]{0:T(256)} %param.9) | copy-start | bytes 3076
  46.8 38.8 %all-to-all-start = ((bf16[16,288,256]{2,1,0:T(8,128)(2,1)}), bf16[16,288,256]{2,1,0:T(8,128)(2,1)S(1)}, u32[]{:S(2)}, u32[]{:S(2)}) async-start(bf16[16,288,256]{2,1,0:T(8,128)(2,1)} %broadcast_in_dim.8), calls=%async_computation | async-start | bytes 4718592 | tf_op jit(solution)/shard_map/all_to_all | solution.py:24
  55.1 140.2 %all-gather.5.cloned.1.call-start = ((), (), s32[]{:S(2)}) async-start(), calls=%async_computation.7 | async-start | bytes 4456448 | tf_op jit(solution)/shard_map/all_gather | solution.py:148
  112.1 4.4 %copy-start.2 = (bf16[4608,768]{1,0:T(8,128)(2,1)S(1)}, bf16[4608,768]{1,0:T(8,128)(2,1)}, u32[]{:S(2)}) copy-start(bf16[4608,768]{1,0:T(8,128)(2,1)} %all-gather.3.cloned.1.call-done) | copy-start | bytes 21233668
  129.3 1.7 slice-start
  195.2 2.2 copy-start
  197.4 9.4 %copy-start.1 = (bf16[2,16,144,256]{3,2,1,0:T(8,128)(2,1)S(1)}, bf16[2,16,144,256]{3,2,1,0:T(8,128)(2,1)}, u32[]{:S(2)}) copy-start(bf16[2,16,144,256]{3,2,1,0:T(8,128)(2,1)} %copy.71) | copy-start | bytes 7077892
  224.6 21.0 %all-to-all-start.3 = ((bf16[8,16,4608]{2,1,0:T(8,128)(2,1)}), bf16[8,16,4608]{2,1,0:T(8,128)(2,1)S(1)}, u32[]{:S(2)}, u32[]{:S(2)}) async-start(bf16[8,16,4608]{2,1,0:T(8,128)(2,1)} %bitcast.15), calls=%async_computation.3 | async-start | bytes 2359296 | tf_op jit(solution)/shard_map/all_to_all | solution.py:175
  230.7 15.3 %copy-start.3 = (f32[4608]{0:T(1024)S(1)}, f32[4608]{0:T(1024)}, u32[]{:S(2)}) copy-start(f32[4608]{0:T(1024)} %param.11) | copy-start | bytes 55300
Sparse Core Ops, SparseCore 0:
  16.2 95.8 all-gather.2
  126.0 69.1 all-gather.4

commit v2 on v1

v2 whole, which is shorter than its diff:
```python
import jax
import jax.numpy as jnp
from jax import lax
from jax.experimental import pallas as pl
from jax.experimental.pallas import tpu as pltpu
from jax.sharding import Mesh
from jax.sharding import PartitionSpec as P

D = 4608
HD = 128
GROUP = 2
SCALAR = 144
DOCS = 8
SEQ = ("xh", "z")
HEAD = ("xl", "y", "c")
PLANE = ("xl", "y")
WIDE = ("xh", "xl", "y")

EPS = 1e-06
CAP = 50.0


def from_everyone(shard, axis):
    copies = jnp.broadcast_to(shard, (lax.axis_size(axis), *shard.shape))
    return lax.all_to_all(copies, axis, split_axis=0, concat_axis=0, tiled=True)


def rotate(values, cosine, sine):
    half = values.shape[1] // 2
    first = values[:, :half]
    second = values[:, half:]
    return jnp.concatenate(
        [first * cosine - second * sine, second * cosine + first * sine], axis=1
    )


def attend_kernel(where_ref, query_ref, start_ref, kv_ref, out_ref, sums, total):
    rows = query_ref.shape[0] // GROUP
    low = where_ref[0]
    own = where_ref[1]
    half = kv_ref.shape[0] // (2 * rows)

    sums[...] = jnp.zeros_like(sums)
    total[...] = jnp.zeros_like(total)
    shape = (GROUP * rows, rows)
    row = lax.broadcasted_iota(jnp.int32, shape, 0)
    index = own * rows + jnp.where(row >= rows, row - rows, row)
    column = lax.broadcasted_iota(jnp.int32, shape, 1)

    @pl.loop(low, own + 1)
    def _(j):
        place = pl.multiple_of((lax.rem(j, 2) * half + lax.div(j, 2)) * rows, rows)
        keys = kv_ref[pl.ds(place, rows), :HD]
        values = kv_ref[pl.ds(place, rows), HD:]
        scores = lax.dot_general(
            query_ref[...], keys, (((1,), (1,)), ((), ())), preferred_element_type=jnp.float32
        )
        weights = jnp.exp(CAP * jnp.tanh(scores * (1.0 / CAP)))
        key_index = j * rows + column
        allowed = (key_index >= start_ref[...]) & (key_index <= index)
        weights = jnp.where(allowed, weights, 0.0)
        part = weights[:, :HD]
        for k in range(1, rows // HD):
            part = part + weights[:, k * HD : (k + 1) * HD]
        sums[...] += part
        total[...] += jnp.dot(
            weights.astype(jnp.bfloat16), values, preferred_element_type=jnp.float32
        )

    result = total[...] / jnp.sum(sums[...], axis=1, keepdims=True)
    for k in range(GROUP):
        out_ref[:, k * HD : (k + 1) * HD] = result[k * rows : (k + 1) * rows].astype(jnp.bfloat16)


def attend(where, stacked, starts, kv):
    rows = stacked.shape[0] // GROUP
    vmem = pl.BlockSpec(memory_space=pltpu.VMEM)
    return pl.pallas_call(
        attend_kernel,
        out_shape=jax.ShapeDtypeStruct((rows, GROUP * HD), jnp.bfloat16),
        in_specs=[pl.BlockSpec(memory_space=pltpu.SMEM), vmem, vmem, vmem],
        out_specs=vmem,
        scratch_shapes=[
            pltpu.VMEM((GROUP * rows, HD), jnp.float32),
            pltpu.VMEM((GROUP * rows, HD), jnp.float32),
        ],
        compiler_params=pltpu.CompilerParams(vmem_limit_bytes=24 * 1024 * 1024),
        cost_estimate=pl.CostEstimate(
            flops=4 * GROUP * rows * HD * kv.shape[0] // 2,
            bytes_accessed=kv.size,
            transcendentals=GROUP * rows * kv.shape[0],
        ),
    )(where, stacked, starts, kv)


def over_plane(shard):
    near = from_everyone(shard[None], WIDE).reshape(-1, *shard.shape)
    return from_everyone(near[None], "c").reshape(2, -1, *shard.shape)


def transposed(block):
    n = lax.axis_size("z")
    pairs = [(z * n + h, h * n + z) for z in range(n) for h in range(n)]
    return lax.ppermute(block, ("z", *HEAD), pairs)


def local(tokens, segments, pre_gain, post_gain, w_query, w_key, w_value, w_out):
    rows, width = tokens.shape
    slab = w_key.shape[0]
    ids = jnp.broadcast_to(segments.astype(jnp.bfloat16)[None, :], (16, rows))
    mine = jnp.concatenate(
        [tokens.T, jnp.concatenate([w_key, w_value], axis=1), w_query, ids], axis=0
    )
    turned = transposed(mine)
    whole = lax.all_gather(turned[:width], "z", axis=0, tiled=True)

    turned, tokens, w_out = lax.optimization_barrier((turned, tokens, w_out))
    seg = turned[-1].astype(jnp.float32)
    levels = jnp.arange(DOCS, dtype=jnp.float32)
    counts = jnp.sum((levels[:, None] > seg[None, :]).astype(jnp.float32), axis=1)
    counts = jnp.zeros((16, 2 * HD), jnp.float32).at[0, :DOCS].set(counts).astype(jnp.bfloat16)
    packed = over_plane(jnp.concatenate([turned[width : width + 2 * slab], counts], axis=0))
    weights = packed[:, :, : 2 * slab].reshape(2, -1, 2, slab, 2 * HD).transpose(2, 1, 0, 3, 4)
    weights = weights.reshape(2, D, 2 * HD)
    starts = jnp.sum(packed[:, :, 2 * slab, :DOCS].astype(jnp.float32), axis=(0, 1))

    onehot = (seg[:, None] == levels[None, :]).astype(jnp.float32)
    tok_start = jnp.sum(onehot * starts[None, :], axis=1)
    block = lax.axis_index(("xh", *HEAD))
    index_f = (block * rows + jnp.arange(rows, dtype=jnp.int32)).astype(jnp.float32)
    position = index_f - tok_start
    half = HD // 2
    freq = 10000.0 ** (-(jnp.arange(half, dtype=jnp.float32) / half))
    angle = position[:, None] * freq[None, :]
    cosine, sine = jnp.cos(angle), jnp.sin(angle)
    start_i = tok_start.astype(jnp.int32)
    where = jnp.stack([start_i[0] // rows, block.astype(jnp.int32)])
    starts_col = jnp.tile(start_i, GROUP)[:, None]

    near = lax.axis_size(PLANE)
    few = rows // (near * 2)
    pieces = tokens.reshape(2, near, few, width).transpose(1, 0, 2, 3).reshape(-1, few, width)
    own = lax.all_to_all(pieces, HEAD, 0, 0, tiled=True).transpose(1, 0, 2).reshape(few, D)

    pair = lax.all_gather(w_out.T, "xh", axis=0, tiled=True)
    whole, own, weights, cosine, sine, pair = lax.optimization_barrier(
        (whole, own, weights, cosine, sine, pair)
    )
    out_t = lax.all_gather(pair, "z", axis=0, tiled=True)

    wide = whole.astype(jnp.float32)
    scale = lax.rsqrt(jnp.mean(wide * wide, axis=0, keepdims=True) + EPS)
    normed = (wide * scale * pre_gain[:, None]).astype(jnp.bfloat16)

    def project(columns):
        return lax.dot_general(
            normed, columns, (((0,), (0,)), ((), ())), preferred_element_type=jnp.float32
        )

    kv = project(weights[0])
    rk = rotate(kv[:, :HD], cosine, sine).astype(jnp.bfloat16)
    vb = kv[:, HD:].astype(jnp.bfloat16)
    kv_own, query_weight = lax.optimization_barrier(
        (jnp.concatenate([rk, vb], axis=1), weights[1])
    )
    kv_all = over_plane(kv_own).reshape(-1, 2 * HD)

    query = project(query_weight)
    stacked = jnp.concatenate(
        [
            (rotate(query[:, k * HD : (k + 1) * HD], cosine, sine) * SCALAR ** (-0.5)).astype(
                jnp.bfloat16
            )
            for k in range(GROUP)
        ],
        axis=0,
    )
    out_t = out_t.reshape(-1, 2, slab, 2 * HD).transpose(1, 0, 2, 3).reshape(D, 2 * HD)

    attn = transposed(attend(where, stacked, starts_col, kv_all))
    partial = lax.dot_general(
        attn, out_t, (((1,), (1,)), ((), ())), preferred_element_type=jnp.float32
    ).astype(jnp.bfloat16)

    halves = lax.all_to_all(partial.reshape(2, rows // 2, D), "c", 0, 0, tiled=True)
    halves = (halves[0].astype(jnp.float32) + halves[1].astype(jnp.float32)).astype(jnp.bfloat16)
    blocks = lax.all_to_all(halves.reshape(near, few, D), PLANE, 0, 0, tiled=True)
    proj = jnp.sum(blocks.astype(jnp.float32), axis=0)
    post = lax.rsqrt(jnp.mean(proj * proj, axis=1, keepdims=True) + EPS)
    result = (own.astype(jnp.float32) + proj * post * post_gain[None, :]).astype(jnp.bfloat16)
    result = from_everyone(result, PLANE).reshape(rows // 2, D)
    return from_everyone(result, "c").reshape(rows, D)


def solution(mesh):
    finer = Mesh(mesh.devices.reshape(2, 16, 2, 4, 2), ("xh", "z", "xl", "y", "c"))
    in_specs = (
        P(SEQ, HEAD),
        P(SEQ),
        P(),
        P(),
        P(SEQ, HEAD),
        P(SEQ, HEAD),
        P(SEQ, HEAD),
        P(HEAD, SEQ),
    )
    return jax.shard_map(
        local, mesh=finer, in_specs=in_specs, out_specs=P(SEQ, None), check_vma=False
    )
```

time: 281 us -> 296 us (1.053)
  the two profiles are of different devices: /device:TPU:37 before, /device:TPU:1 now
where the time goes in v2:
time: 296 us
  blocking collectives  121 us (41%)
  starting transfers between devices  70.5 us (24%)
  waiting for transfers between devices  54 us (18%)
  local copies, waits for them, and re-layouts  17.9 us (6%)
  between operations  16.5 us (6%)
  matrix products  7.95 us (3%)
  other arithmetic  6.13 us (2%)
    all_to_all x1, starting transfers between devices, local(): lax.all_to_all(pieces, HEAD, 0, 0, tiled=True).transpose(1, 0, 2)  53.6 us
    all_to_all x4, blocking collectives, from_everyone(): return lax.all_to_all(copies, axis, split_axis=0, concat_axis=0, tiled=True)  51.7 us
    all_gather x1, blocking collectives, local(): pair = lax.all_gather(w_out.T, 'xh', axis=0, tiled=True)  35.3 us
    all_gather x1, waiting for transfers between devices, local(): out_t = lax.all_gather(pair, 'z', axis=0, tiled=True)  30.4 us
    all_to_all x1, blocking collectives, local(): lax.all_to_all(halves.reshape(near, few, D), PLANE, 0, 0, tiled=True)  21 us
    all_to_all x1, blocking collectives, local(): lax.all_to_all(partial.reshape(2, rows // 2, D), 'c', 0, 0, tiled=True)  13.1 us
    all_to_all x2, waiting for transfers between devices, from_everyone(): return lax.all_to_all(copies, axis, split_axis=0, concat_axis=0, tiled=True)  11.8 us
    all_to_all x2, starting transfers between devices, from_everyone(): return lax.all_to_all(copies, axis, split_axis=0, concat_axis=0, tiled=True)  10 us
  transfers between devices with their start and end apart: 7, of which 4 were waited for; matrix products, arithmetic and copies ran while one was open for 8% of the time, Pallas kernels for 1%

profile of v2, /device:TPU:1, one launch (start us, length us, event | category | flops | bytes accessed | tf_op | source)
XLA Modules:
  0.0 295.8 jit_solution(8060058975526478894)
XLA Ops:
  6.5 0.7 convert_element_type.76
  7.2 1.0 pad_maximum_fusion
  8.2 4.9 %collective-permute-start = (bf16[592,256]{1,0:T(8,128)(2,1)S(1)}, bf16[592,256]{1,0:T(8,128)(2,1)S(1)}, u32[]{:S(2)}, u32[]{:S(2)}) collective-permute-start(bf16[592,256]{1,0:T(8,128)(2,1)S(1)} %pad_maximum_fusion), channel_id=1, source_target_pairs={{0,0},{1,16},{2,32},{3,48},{4,64},{5,80},{6,96},{7,112},{8,128},{9... | collective-permute-start | bytes 909320 | tf_op jit(solution)/shard_map/ppermute | solution.py:104
  13.2 5.2 %collective-permute-done = bf16[592,256]{1,0:T(8,128)(2,1)S(1)} collective-permute-done((bf16[592,256]{1,0:T(8,128)(2,1)S(1)}, bf16[592,256]{1,0:T(8,128)(2,1)S(1)}, u32[]{:S(2)}, u32[]{:S(2)}) %collective-permute-start) | collective-permute-done | bytes 303136 | tf_op jit(solution)/shard_map/ppermute | solution.py:104
  18.4 0.7 slice.94
  19.1 0.0 all-gather.3.cloned.1.call-update
  19.1 1.1 copy.60
  20.2 0.7 copy.61
  20.9 53.6 %all-to-all-start = ((bf16[16,16,288]{2,1,0:T(8,128)(2,1)}), bf16[16,16,288]{2,1,0:T(8,128)(2,1)S(1)}, u32[]{:S(2)}, u32[]{:S(2)}) async-start(bf16[16,16,288]{2,1,0:T(8,128)(2,1)} %bitcast.3), calls=%async_computation | async-start | bytes 393216 | tf_op jit(solution)/shard_map/all_to_all | solution.py:143
  74.5 0.1 convert_reduce_fusion.1
  74.6 6.5 %all-to-all-done = bf16[16,16,288]{2,1,0:T(8,128)(2,1)S(1)} async-done(((bf16[16,16,288]{2,1,0:T(8,128)(2,1)}), bf16[16,16,288]{2,1,0:T(8,128)(2,1)S(1)}, u32[]{:S(2)}, u32[]{:S(2)}) %all-to-all-start) | async-done | bytes 147488 | tf_op jit(solution)/shard_map/all_to_all | solution.py:143
  81.1 1.6 broadcast_in_dim.15
  82.7 5.2 %all-to-all-start.1 = ((bf16[16,1,304,256]{3,2,1,0:T(8,128)(2,1)}), bf16[16,1,304,256]{3,2,1,0:T(8,128)(2,1)S(1)}, u32[]{:S(2)}, u32[]{:S(2)}) async-start(bf16[16,1,304,256]{3,2,1,0:T(8,128)(2,1)} %broadcast_in_dim.15), calls=%async_computation.1 | async-start | bytes 4980736 | tf_op jit(solution)/shard_map/all_to_all | solution.py:25
  88.0 0.0 all-gather.5.cloned.1.call-start
  88.0 35.3 %all_gather.10 = bf16[288,256]{1,0:T(8,128)(2,1)} all-gather(bf16[144,256]{1,0:T(8,128)(2,1)S(1)} %bitcast.61), channel_id=1, replica_groups=mesh['xh'=2,'z'=16,'xl'=2,'y'=4,'c'=2] {'xh'}, dimensions={0}, use_global_device_ids=true | all-gather | bytes 221184 | tf_op jit(solution)/shard_map/all_gather | solution.py:145
  123.4 0.2 reshape.122
  123.6 0.0 all-to-all-done.1
  123.6 0.3 broadcast_in_dim.16
  124.0 9.0 %all_to_all.45 = bf16[2,1,16,304,256]{4,3,2,1,0:T(8,128)(2,1)S(1)} all-to-all(bf16[2,1,16,304,256]{4,3,2,1,0:T(8,128)(2,1)S(1)} %broadcast_in_dim.16), channel_id=1, replica_groups=mesh['xh'=2,'z'=16,'xl'=2,'y'=4,'c'=2] {'c'}, dimensions={0} | all-to-all | bytes 9961472 | tf_op jit(solution)/shard_map/all_to_all | solution.py:25
  132.9 0.6 slice.95
  133.5 2.7 copy.63
  136.2 0.1 fusion.13
  136.2 0.1 select_reduce_fusion
  136.3 0.5 multiply_sine_fusion
  136.9 0.0 all-gather.3.cloned.1.call-done
  136.9 2.5 fusion
  139.4 0.0 all-gather.5.cloned.1.call-update
  139.4 3.2 %fusion.3 = f32[256,256]{0,1:T(8,128)S(1)} fusion(bf16[2,4608,256]{2,1,0:T(8,128)(2,1)} %bitcast.48, bf16[4608,256]{1,0:T(8,128)(2,1)S(1)} %copy-done, f32[4608]{0:T(1024)S(1)} %copy-done.3, f32[256]{0:T(256)S(1)} %add_rsqrt_fusion), kind=kOutput, calls=%fused_computation.6 | convolution fusion | flops 608698368 | bytes 5000192 | tf_op jit(solution)/shard_map/dot_general | solution.py:156
  142.6 0.1 copy.77
  142.7 0.1 copy.76
  142.8 0.1 subtract_convert_fusion
  142.9 0.1 copy.67
  143.0 0.1 copy.66
  143.1 3.2 %slice_bitcast_fusion = bf16[4608,256]{1,0:T(8,128)(2,1)} fusion(bf16[2,4608,256]{2,1,0:T(8,128)(2,1)} %bitcast.49), kind=kLoop, calls=%fused_computation.10 | loop fusion | bytes 4718592 | tf_op jit(solution)/shard_map/squeeze | solution.py:164
  146.3 0.1 copy.72
  146.4 1.6 broadcast_in_dim.17
  148.0 4.8 %all-to-all-start.3 = ((bf16[16,1,256,256]{3,2,1,0:T(8,128)(2,1)}), bf16[16,1,256,256]{3,2,1,0:T(8,128)(2,1)S(1)}, u32[]{:S(2)}, u32[]{:S(2)}) async-start(bf16[16,1,256,256]{3,2,1,0:T(8,128)(2,1)} %broadcast_in_dim.17), calls=%async_computation.3 | async-start | bytes 4194304 | tf_op jit(solution)/shard_map/all_to_all | solution.py:25
  152.8 0.6 slice.82
  156.1 0.1 copy.79
  156.3 0.1 pad_add_fusion.where_ref
  156.4 4.0 %fusion.6 = f32[256,256]{1,0:T(8,128)S(1)} fusion(bf16[4608,256]{1,0:T(8,128)(2,1)} %slice_bitcast_fusion, bf16[4608,256]{1,0:T(8,128)(2,1)} %all-gather.3.cloned.1.call-done, f32[4608]{0:T(1024)S(1)} %copy-done.3, f32[256]{0:T(256)S(1)} %add_rsqrt_fusion), kind=kOutput, calls=%fused_computation.12 | convolution fusion | flops 608698368 | bytes 5000192 | tf_op jit(solution)/shard_map/dot_general | solution.py:156
  160.4 0.2 multiply_subtract_fusion.1
  160.5 0.1 fusion.11
  160.7 11.8 %all-to-all-done.3 = bf16[16,1,256,256]{3,2,1,0:T(8,128)(2,1)S(1)} async-done(((bf16[16,1,256,256]{3,2,1,0:T(8,128)(2,1)}), bf16[16,1,256,256]{3,2,1,0:T(8,128)(2,1)S(1)}, u32[]{:S(2)}, u32[]{:S(2)}) %all-to-all-start.3) | async-done | bytes 2097184 | tf_op jit(solution)/shard_map/all_to_all | solution.py:25
  172.5 0.5 broadcast_in_dim.18
  173.0 16.5 %all_to_all.46 = bf16[2,1,16,256,256]{4,3,2,1,0:T(8,128)(2,1)S(1)} all-to-all(bf16[2,1,16,256,256]{4,3,2,1,0:T(8,128)(2,1)S(1)} %broadcast_in_dim.18), channel_id=1, replica_groups=mesh['xh'=2,'z'=16,'xl'=2,'y'=4,'c'=2] {'c'}, dimensions={0} | all-to-all | bytes 8388608 | tf_op jit(solution)/shard_map/all_to_all | solution.py:25
  189.4 1.7 shard_map.82
  191.1 2.0 collective-permute-start.1
  193.1 30.4 %all-gather.5.cloned.1.call-done = bf16[4608,256]{1,0:T(8,128)(2,1)} async-done(((bf16[288,256]{1,0:T(8,128)(2,1)}), bf16[4608,256]{1,0:T(8,128)(2,1)}) %all-gather.5.cloned.1.call-update) | async-done | bytes 2359312 | tf_op jit(solution)/shard_map/all_gather | solution.py:149
  223.5 1.8 copy.74
  225.3 0.0 collective-permute-done.1
  225.3 0.8 convolution_convert_fusion
  226.2 13.1 %all_to_all.47 = bf16[2,128,4608]{2,1,0:T(8,128)(2,1)S(1)} all-to-all(bf16[2,128,4608]{2,1,0:T(8,128)(2,1)S(1)} %bitcast.52), channel_id=1, replica_groups=mesh['xh'=2,'z'=16,'xl'=2,'y'=4,'c'=2] {'c'}, dimensions={0} | all-to-all | bytes 4718592 | tf_op jit(solution)/shard_map/all_to_all | solution.py:185
  239.3 0.3 add_convert_fusion
  239.6 0.0 copy-start.2
  239.6 21.0 %all_to_all.48 = bf16[8,16,4608]{2,1,0:T(8,128)(2,1)S(1)} all-to-all(bf16[8,16,4608]{2,1,0:T(8,128)(2,1)S(1)} %bitcast.55), channel_id=1, replica_groups=mesh['xh'=2,'z'=16,'xl'=2,'y'=4,'c'=2] {'xl','y'}, dimensions={0} | all-to-all | bytes 2359296 | tf_op jit(solution)/shard_map/all_to_all | solution.py:187
  260.6 0.2 convert_reduce_fusion
  260.7 0.2 multiply_reduce_fusion
  260.9 0.1 add_convert_fusion.1
  261.0 0.1 broadcast_in_dim.19
  261.1 18.1 %all_to_all.49 = bf16[8,16,4608]{2,1,0:T(8,128)(2,1)S(1)} all-to-all(bf16[8,16,4608]{2,1,0:T(8,128)(2,1)S(1)} %broadcast_in_dim.19), channel_id=1, replica_groups=mesh['xh'=2,'z'=16,'xl'=2,'y'=4,'c'=2] {'xl','y'}, dimensions={0} | all-to-all | bytes 2359296 | tf_op jit(solution)/shard_map/all_to_all | solution.py:25
  279.2 0.2 broadcast_in_dim.20
  279.3 8.2 %all_to_all.50 = bf16[2,128,4608]{2,1,0:T(8,128)(2,1)S(1)} all-to-all(bf16[2,128,4608]{2,1,0:T(8,128)(2,1)S(1)} %broadcast_in_dim.20), channel_id=1, replica_groups=mesh['xh'=2,'z'=16,'xl'=2,'y'=4,'c'=2] {'c'}, dimensions={0} | all-to-all | bytes 4718592 | tf_op jit(solution)/shard_map/all_to_all | solution.py:25
  287.5 1.4 copy.81
  (23 shorter events, 0.2 us)
Async XLA Ops:
  6.5 130.4 %all-gather.3.cloned.1.call-start = ((), (), s32[]{:S(2)}) async-start(), calls=%async_computation.9 | async-start | bytes 2506752 | tf_op jit(solution)/shard_map/all_gather | solution.py:115
  8.2 10.2 %collective-permute-start = (bf16[592,256]{1,0:T(8,128)(2,1)S(1)}, bf16[592,256]{1,0:T(8,128)(2,1)S(1)}, u32[]{:S(2)}, u32[]{:S(2)}) collective-permute-start(bf16[592,256]{1,0:T(8,128)(2,1)S(1)} %pad_maximum_fusion), channel_id=1, source_target_pairs={{0,0},{1,16},{2,32},{3,48},{4,64},{5,80},{6,96},{7,112},{8,128},{9... | collective-permute-start | bytes 909320 | tf_op jit(solution)/shard_map/ppermute | solution.py:104
  20.9 60.2 %all-to-all-start = ((bf16[16,16,288]{2,1,0:T(8,128)(2,1)}), bf16[16,16,288]{2,1,0:T(8,128)(2,1)S(1)}, u32[]{:S(2)}, u32[]{:S(2)}) async-start(bf16[16,16,288]{2,1,0:T(8,128)(2,1)} %bitcast.3), calls=%async_computation | async-start | bytes 393216 | tf_op jit(solution)/shard_map/all_to_all | solution.py:143
  82.7 5.3 %copy-start.1 = (bf16[256,144]{0,1:T(8,128)(2,1)S(1)}, bf16[256,144]{0,1:T(8,128)(2,1)}, u32[]{:S(2)}) copy-start(bf16[256,144]{0,1:T(8,128)(2,1)} %param.17) | copy-start | bytes 221188
  82.7 40.9 %all-to-all-start.1 = ((bf16[16,1,304,256]{3,2,1,0:T(8,128)(2,1)}), bf16[16,1,304,256]{3,2,1,0:T(8,128)(2,1)S(1)}, u32[]{:S(2)}, u32[]{:S(2)}) async-start(bf16[16,1,304,256]{3,2,1,0:T(8,128)(2,1)} %broadcast_in_dim.15), calls=%async_computation.1 | async-start | bytes 4980736 | tf_op jit(solution)/shard_map/all_to_all | solution.py:25
  88.0 135.5 %all-gather.5.cloned.1.call-start = ((), (), s32[]{:S(2)}) async-start(), calls=%async_computation.10 | async-start | bytes 2506752 | tf_op jit(solution)/shard_map/all_gather | solution.py:149
  136.2 3.2 %copy-start.3 = (f32[4608]{0:T(1024)S(1)}, f32[4608]{0:T(1024)}, u32[]{:S(2)}) copy-start(f32[4608]{0:T(1024)} %param.12) | copy-start | bytes 55300
  136.9 2.5 copy-start
  148.0 24.5 %all-to-all-start.3 = ((bf16[16,1,256,256]{3,2,1,0:T(8,128)(2,1)}), bf16[16,1,256,256]{3,2,1,0:T(8,128)(2,1)S(1)}, u32[]{:S(2)}, u32[]{:S(2)}) async-start(bf16[16,1,256,256]{3,2,1,0:T(8,128)(2,1)} %broadcast_in_dim.17), calls=%async_computation.3 | async-start | bytes 4194304 | tf_op jit(solution)/shard_map/all_to_all | solution.py:25
  191.1 34.2 %collective-permute-start.1 = (bf16[256,256]{1,0:T(8,128)(2,1)S(1)}, bf16[256,256]{1,0:T(8,128)(2,1)S(1)}, u32[]{:S(2)}, u32[]{:S(2)}) collective-permute-start(bf16[256,256]{1,0:T(8,128)(2,1)S(1)} %shard_map.82), channel_id=1, source_target_pairs={{0,0},{1,16},{2,32},{3,48},{4,64},{5,80},{6,96},{7,112},{8,128},{9... | collective-permute-start | bytes 393224 | tf_op jit(solution)/shard_map/ppermute | solution.py:104
  239.6 21.3 %copy-start.2 = (f32[4608]{0:T(1024)S(1)}, f32[4608]{0:T(1024)}, u32[]{:S(2)}) copy-start(f32[4608]{0:T(1024)} %param.13) | copy-start | bytes 55300
Sparse Core Ops, SparseCore 0:
  19.2 113.6 all-gather.2
  139.5 83.9 all-gather.4

commit v3 on v1

--- a/solution.py
+++ b/solution.py
@@ -101,7 +101,7 @@
             pltpu.VMEM((GROUP * rows, HD), jnp.float32),
             pltpu.SemaphoreType.DMA((blocks,)),
         ],
-        compiler_params=pltpu.CompilerParams(vmem_limit_bytes=24 * 1024 * 1024),
+        compiler_params=pltpu.CompilerParams(vmem_limit_bytes=60 * 1024 * 1024),
         cost_estimate=pl.CostEstimate(
             flops=4 * GROUP * rows * HD * kv.shape[0] // 2,
             bytes_accessed=kv.size,
@@ -111,59 +111,83 @@
 
 
 def local(tokens, segments, pre_gain, post_gain, w_query, w_key, w_value, w_out):
-    rows = tokens.shape[0]
+    rows, width = tokens.shape
     deep = lax.axis_size("z")
-    slab = w_key.shape[0]
     mine = jnp.concatenate([w_key, w_value, w_query, w_out.T], axis=1)
-    pair = lax.all_gather(mine, "xh", axis=0, tiled=True)
-    weights = lax.all_gather(pair, "z", axis=0, tiled=True)
-
-    whole = from_everyone(tokens.T, HEAD).reshape(D, rows)
-    wide = whole.astype(jnp.float32)
-    scale = lax.rsqrt(jnp.mean(wide * wide, axis=0, keepdims=True) + EPS)
-    normed = (wide * scale * pre_gain[:, None]).astype(jnp.bfloat16)
-    normed = normed.reshape(2, deep, slab, rows).transpose(1, 0, 2, 3).reshape(D, rows).T
-    normed = lax.optimization_barrier(normed)
-
-    levels = jnp.arange(DOCS, dtype=jnp.int32)
-    counts = jnp.sum((levels[None, :] > segments[:, None]).astype(jnp.float32), axis=0)
-    starts = jnp.sum(from_everyone(counts, SEQ).reshape(-1, DOCS), axis=0)
-    onehot = (segments[:, None] == levels[None, :]).astype(jnp.float32)
-    tok_start = jnp.sum(onehot * starts[None, :], axis=1)
-    block = lax.axis_index(SEQ)
-    index_f = (block * rows + jnp.arange(rows, dtype=jnp.int32)).astype(jnp.float32)
-    position = index_f - tok_start
+    weights = lax.all_gather(mine, "z", axis=0, tiled=True)
+    deep_half = weights.shape[0]
+
+    ids = jnp.broadcast_to(segments.astype(jnp.bfloat16)[None, :], (16, rows))
+    slices = jnp.concatenate([tokens.T, ids], axis=0)
+    slices = lax.ppermute(slices, ("xh", "xl"), [(0, 0), (1, 2), (2, 1), (3, 3)])
+    slices = from_everyone(slices[None], PLANE).reshape(-1, *slices.shape)
+    slices = from_everyone(slices[None], "c").reshape(2, 2, -1, *slices.shape[1:])
+    seg = slices[0, :, 0, width].astype(jnp.float32)
+    levels = jnp.arange(DOCS, dtype=jnp.float32)
+    counts = jnp.sum((levels[:, None, None] > seg[None]).astype(jnp.float32), axis=(1, 2))
+    starts = jnp.sum(from_everyone(counts[None], "z").reshape(-1, DOCS), axis=0)
+    onehot = (seg[:, :, None] == levels).astype(jnp.float32)
+    tok_start = jnp.sum(onehot * starts, axis=2)
+    side = lax.axis_index("xh")
+    place = lax.axis_index("z")
+    blocks = (jnp.arange(2, dtype=jnp.int32) * deep + place)[:, None] * rows
+    index_f = (blocks + jnp.arange(rows, dtype=jnp.int32)).astype(jnp.float32)
+    position = (index_f - tok_start).reshape(2 * rows)
     half = HD // 2
     freq = 10000.0 ** (-(jnp.arange(half, dtype=jnp.float32) / half))
     angle = position[:, None] * freq[None, :]
     cosine, sine = jnp.cos(angle), jnp.sin(angle)
-    start_i = tok_start.astype(jnp.int32)
-    where = jnp.stack([start_i[0] // rows, block.astype(jnp.int32), jnp.int32(deep)])
+    start_i = lax.dynamic_index_in_dim(tok_start, side, 0, keepdims=False).astype(jnp.int32)
+    where = jnp.stack(
+        [start_i[0] // rows, (side * deep + place).astype(jnp.int32), jnp.int32(deep)]
+    )
     starts_col = jnp.tile(start_i, GROUP)[:, None]
 
-    kv = jnp.dot(normed, weights[:, : 2 * HD], preferred_element_type=jnp.float32)
+    wide = slices[:, :, :, :width].transpose(1, 2, 0, 3, 4).reshape(2, deep_half, rows)
+    wide = wide.astype(jnp.float32)
+    squares = jnp.sum(lax.all_gather(jnp.sum(wide * wide, axis=1), "xh", axis=0), axis=0)
+    scale = lax.rsqrt(squares / D + EPS)
+    gain = lax.dynamic_slice_in_dim(pre_gain, side * deep_half, deep_half, 0)
+    normed = (wide * scale[:, None, :] * gain[None, :, None]).astype(jnp.bfloat16)
+    normed = normed.transpose(0, 2, 1).reshape(2 * rows, deep_half)
+    normed, cosine, sine, weights = lax.optimization_barrier((normed, cosine, sine, weights))
+
+    def project(columns):
+        part = jnp.dot(normed, columns, preferred_element_type=jnp.float32).astype(jnp.bfloat16)
+        both = lax.all_gather(part, "xh", axis=0)
+        return both[0].astype(jnp.float32) + both[1].astype(jnp.float32)
+
+    kv = project(weights[:, : 2 * HD])
     rk = rotate(kv[:, :HD], cosine, sine).astype(jnp.bfloat16)
     vb = kv[:, HD:].astype(jnp.bfloat16)
-    kv_pair = lax.all_gather(jnp.concatenate([rk, vb], axis=1), "xh", axis=0, tiled=True)
+    kv_pair, query_weight, out_weight, tokens = lax.optimization_barrier(
+        (
+            jnp.concatenate([rk, vb], axis=1),
+            weights[:, 2 * HD : 4 * HD],
+            weights[:, 4 * HD :],
+            tokens,
+        )
+    )
     kv_all = lax.all_gather(kv_pair, "z", axis=0, tiled=True)
 
-    query = jnp.dot(normed, weights[:, 2 * HD : 4 * HD], preferred_element_type=jnp.float32)
+    query = lax.dynamic_slice_in_dim(project(query_weight), side * rows, rows, 0)
+    own_cos = lax.dynamic_slice_in_dim(cosine, side * rows, rows, 0)
+    own_sin = lax.dynamic_slice_in_dim(sine, side * rows, rows, 0)
     stacked = jnp.concatenate(
         [
-            (rotate(query[:, k * HD : (k + 1) * HD], cosine, sine) * SCALAR ** (-0.5)).astype(
+            (rotate(query[:, k * HD : (k + 1) * HD], own_cos, own_sin) * SCALAR ** (-0.5)).astype(
                 jnp.bfloat16
             )
             for k in range(GROUP)
         ],
         axis=0,
     )
-    out_t = weights[:, 4 * HD :].reshape(deep, 2, slab, GROUP * HD).transpose(1, 0, 2, 3)
-    out_t = lax.optimization_barrier(out_t.reshape(D, GROUP * HD))
-
+    out_t = from_everyone(out_weight[None], "xh").reshape(D, GROUP * HD)
     near = lax.axis_size(PLANE)
-    few = rows // (near * lax.axis_size("c"))
-    first_row = (lax.axis_index("c") * near + lax.axis_index(PLANE)) * few
-    own = lax.dynamic_slice_in_dim(whole, first_row, few, 1).T.astype(jnp.float32)
+    few = rows // (near * 2)
+    pieces = tokens.reshape(2, near, few, width).transpose(1, 0, 2, 3).reshape(-1, few, width)
+    own = lax.all_to_all(pieces, HEAD, 0, 0, tiled=True).transpose(1, 0, 2).reshape(few, D)
+    kv_all, stacked, out_t, own = lax.optimization_barrier((kv_all, stacked, out_t, own))
 
     attn = attend(where, stacked, starts_col, kv_all)
     partial = lax.dot_general(
@@ -175,7 +199,7 @@
     pieces = lax.all_to_all(halves.reshape(near, few, D), PLANE, 0, 0, tiled=True)
     proj = jnp.sum(pieces.astype(jnp.float32), axis=0)
     post = lax.rsqrt(jnp.mean(proj * proj, axis=1, keepdims=True) + EPS)
-    result = (own + proj * post * post_gain[None, :]).astype(jnp.bfloat16)
+    result = (own.astype(jnp.float32) + proj * post * post_gain[None, :]).astype(jnp.bfloat16)
     result = from_everyone(result, PLANE).reshape(rows // 2, D)
     return from_everyone(result, "c").reshape(rows, D)
 

time: 281 us -> 254 us (0.904)
  waiting for transfers between devices: 130 us -> 46.2 us
  starting transfers between devices: 12.9 us -> 42 us
  blocking collectives: 84.6 us -> 110 us
  other arithmetic: 5.99 us -> 9.76 us
    all_gather x1, waiting for transfers between devices: 62.6 us -> 13.5 us  [local(): kv_all = lax.all_gather(kv_pair, 'z', axis=0, tiled=True)]
    all_gather x2 -> x3, blocking collectives: 14.7 us -> 40.8 us  [the longest x2 36.1 us: project(): both = lax.all_gather(part, 'xh', axis=0)]
    all_to_all x3, blocking collectives: 54.2 us -> 32.6 us  [from_everyone(): return lax.all_to_all(copies, axis, split_axis=0, concat_axis=0, tiled=True)]
    all_to_all x0 -> x1, blocking collectives: none -> 20.5 us  [local(): lax.all_to_all(halves.reshape(near, few, D), PLANE, 0, 0, tiled=True)]
    all_gather x1, waiting for transfers between devices: 23.4 us -> 7.85 us  [local(): weights = lax.all_gather(mine, 'z', axis=0, tiled=True)]
    all_to_all x1 -> x3, starting transfers between devices: 8.26 us -> 23.3 us  [from_everyone(): return lax.all_to_all(copies, axis, split_axis=0, concat_axis=0, tiled=True)]
    all_to_all x1 -> x3, waiting for transfers between devices: 30.3 us -> 18.1 us  [from_everyone(): return lax.all_to_all(copies, axis, split_axis=0, concat_axis=0, tiled=True)]
    all_to_all x1, starting transfers between devices: 4.62 us -> 16.4 us  [local(): lax.all_to_all(pieces, HEAD, 0, 0, tiled=True).transpose(1, 0, 2)]
  transfers between devices with their start and end apart: 4 -> 7, of which waited for: 4 -> 6; matrix products, arithmetic and copies ran while one was open for 4% -> 7% of each run, Pallas kernels for 0% -> 0%
where the time goes in v3:
time: 254 us; the launch traced here: 253 us
  blocking collectives  110 us (43%)
  waiting for transfers between devices  46.2 us (18%)
  starting transfers between devices  42 us (17%)
  between operations  16.2 us (6%)
  local copies, waits for them, and re-layouts  13.3 us (5%)
  Pallas kernels  9.92 us (4%)
  other arithmetic  9.76 us (4%)
  matrix products  6.52 us (3%)
    all_gather x2, blocking collectives, project(): both = lax.all_gather(part, 'xh', axis=0)  36.1 us
    all_to_all x3, blocking collectives, from_everyone(): return lax.all_to_all(copies, axis, split_axis=0, concat_axis=0, tiled=True)  32.6 us
    all_to_all x3, starting transfers between devices, from_everyone(): return lax.all_to_all(copies, axis, split_axis=0, concat_axis=0, tiled=True)  23.3 us
    all_to_all x1, blocking collectives, local(): lax.all_to_all(halves.reshape(near, few, D), PLANE, 0, 0, tiled=True)  20.5 us
    all_to_all x3, waiting for transfers between devices, from_everyone(): return lax.all_to_all(copies, axis, split_axis=0, concat_axis=0, tiled=True)  18.1 us
    all_to_all x1, starting transfers between devices, local(): lax.all_to_all(pieces, HEAD, 0, 0, tiled=True).transpose(1, 0, 2)  16.4 us
    all_to_all x1, blocking collectives, local(): lax.all_to_all(partial.reshape(2, rows // 2, D), 'c', 0, 0, tiled=True)  15.6 us
    all_gather x1, waiting for transfers between devices, local(): kv_all = lax.all_gather(kv_pair, 'z', axis=0, tiled=True)  13.5 us
  transfers between devices with their start and end apart: 7, of which 6 were waited for; matrix products, arithmetic and copies ran while one was open for 7% of the time, Pallas kernels for 0%

profile of v3, /device:TPU:37, one launch (start us, length us, event | category | flops | bytes accessed | tf_op | source)
XLA Modules:
  0.0 253.5 jit_solution(6985056250579356924)
XLA Ops:
  6.5 1.6 pad_maximum_fusion.1
  8.2 0.0 all-gather.7.cloned.1.call-update
  8.2 0.7 convert_element_type.109
  8.9 0.9 pad_maximum_fusion.2
  9.8 2.2 collective-permute-start
  12.0 4.6 %collective-permute-done = bf16[304,256]{1,0:T(8,128)(2,1)S(1)} collective-permute-done((bf16[304,256]{1,0:T(8,128)(2,1)S(1)}, bf16[304,256]{1,0:T(8,128)(2,1)S(1)}, u32[]{:S(2)}, u32[]{:S(2)}) %collective-permute-start) | collective-permute-done | bytes 155680 | tf_op jit(solution)/shard_map/ppermute | solution.py:122
  16.6 1.1 broadcast_in_dim.15
  17.7 4.2 %all-to-all-start = ((bf16[8,1,304,256]{3,2,1,0:T(8,128)(2,1)}), bf16[8,1,304,256]{3,2,1,0:T(8,128)(2,1)S(1)}, u32[]{:S(2)}, u32[]{:S(2)}) async-start(bf16[8,1,304,256]{3,2,1,0:T(8,128)(2,1)} %broadcast_in_dim.15), calls=%async_computation | async-start | bytes 2490368 | tf_op jit(solution)/shard_map/all_to_all | solution.py:24
  21.9 0.1 dynamic_slice.18
  22.0 16.8 %all-to-all-done = bf16[8,1,304,256]{3,2,1,0:T(8,128)(2,1)S(1)} async-done(((bf16[8,1,304,256]{3,2,1,0:T(8,128)(2,1)}), bf16[8,1,304,256]{3,2,1,0:T(8,128)(2,1)S(1)}, u32[]{:S(2)}, u32[]{:S(2)}) %all-to-all-start) | async-done | bytes 1245216 | tf_op jit(solution)/shard_map/all_to_all | solution.py:24
  38.8 0.2 broadcast_in_dim.16
  39.0 6.4 %all_to_all.45 = bf16[2,1,8,304,256]{4,3,2,1,0:T(8,128)(2,1)S(1)} all-to-all(bf16[2,1,8,304,256]{4,3,2,1,0:T(8,128)(2,1)S(1)} %broadcast_in_dim.16), channel_id=1, replica_groups=mesh['xh'=2,'z'=16,'xl'=2,'y'=4,'c'=2] {'c'}, dimensions={0} | all-to-all | bytes 4980736 | tf_op jit(solution)/shard_map/all_to_all | solution.py:24
  45.3 0.2 copy.30
  45.5 0.1 convert_reduce_fusion.1
  45.6 0.6 broadcast_in_dim.17
  46.2 14.7 %all-to-all-start.2 = ((f32[16,1,8]{2,1,0:T(1,128)}), f32[16,1,8]{2,1,0:T(1,128)S(1)}, u32[]{:S(2)}, u32[]{:S(2)}) async-start(f32[16,1,8]{2,1,0:T(1,128)} %broadcast_in_dim.17), calls=%async_computation.2 | async-start | bytes 16384 | tf_op jit(solution)/shard_map/all_to_all | solution.py:24
  60.9 0.0 all-gather.9.cloned.1.call-start
  60.9 0.5 multiply_reduce_fusion
  61.4 4.7 %all-gather.3 = f32[2,2,256]{2,1,0:T(2,128)S(1)} all-gather(f32[1,2,256]{2,1,0:T(2,128)S(1)} %bitcast.66), channel_id=2, replica_groups=mesh['xh'=2,'z'=16,'xl'=2,'y'=4,'c'=2] {'xh'}, dimensions={0}, use_global_device_ids=true | all-gather | bytes 6144 | tf_op jit(solution)/shard_map/all_gather | solution.py:148
  66.2 0.5 slice_convert_fusion
  66.7 0.8 fusion.1
  67.5 2.4 copy.31
  69.9 1.4 all-to-all-done.2
  71.3 0.1 select_reduce_fusion
  71.4 0.1 subtract_bitcast_fusion
  71.5 1.0 multiply_sine_fusion
  72.5 7.8 %all-gather.7.cloned.1.call-done = bf16[2304,768]{1,0:T(8,128)(2,1)} async-done(((bf16[144,768]{1,0:T(8,128)(2,1)}), bf16[2304,768]{1,0:T(8,128)(2,1)}) %all-gather.7.cloned.1.call-update) | async-done | bytes 3538960 | tf_op jit(solution)/shard_map/all_gather | solution.py:117
  80.3 3.0 %fusion.6 = (bf16[2304,256]{1,0:T(8,128)(2,1)S(1)}, bf16[2304,256]{1,0:T(8,128)(2,1)}) fusion(bf16[2304,768]{1,0:T(8,128)(2,1)} %all-gather.7.cloned.1.call-done), kind=kLoop, calls=%fused_computation.47 | loop fusion | bytes 4718592 | tf_op jit(solution)/shard_map/slice | solution.py:167
  83.3 2.0 convolution_convert_fusion.2
  85.3 0.0 copy-start.1
  85.3 7.5 %all-gather.1 = bf16[1024,256]{1,0:T(8,128)(2,1)S(1)} all-gather(bf16[512,256]{1,0:T(8,128)(2,1)S(1)} %convolution_convert_fusion.2), channel_id=3, replica_groups=mesh['xh'=2,'z'=16,'xl'=2,'y'=4,'c'=2] {'xh'}, dimensions={0}, use_global_device_ids=true | all-gather | bytes 786432 | tf_op jit(solution)/shard_map/all_gather | solution.py:157
  92.9 0.1 convert_add_fusion
  92.9 0.2 subtract_convert_fusion
  93.1 0.9 pad_maximum_fusion
  94.0 0.0 all-gather.9.cloned.1.call-update
  94.0 0.2 copy.33
  94.2 0.7 copy.34
  94.9 16.4 %all-to-all-start.4 = ((bf16[16,16,288]{2,1,0:T(8,128)(2,1)}), bf16[16,16,288]{2,1,0:T(8,128)(2,1)S(1)}, u32[]{:S(2)}, u32[]{:S(2)}) async-start(bf16[16,16,288]{2,1,0:T(8,128)(2,1)} %bitcast.12), calls=%async_computation.4 | async-start | bytes 393216 | tf_op jit(solution)/shard_map/all_to_all | solution.py:189
  111.3 0.5 slice.104
  114.4 0.9 copy.41
  115.3 0.6 pad_add_fusion.where_ref
  115.9 2.1 all-to-all-done.4
  118.0 1.6 broadcast_in_dim.18
  119.6 4.5 %all-to-all-start.3 = ((bf16[2,1,2304,256]{3,2,1,0:T(8,128)(2,1)}), bf16[2,1,2304,256]{3,2,1,0:T(8,128)(2,1)S(1)}, u32[]{:S(2)}, u32[]{:S(2)}) async-start(bf16[2,1,2304,256]{3,2,1,0:T(8,128)(2,1)} %broadcast_in_dim.18), calls=%async_computation.3 | async-start | bytes 4718592 | tf_op jit(solution)/shard_map/all_to_all | solution.py:24
  124.0 2.8 %convolution_convert_fusion.1 = bf16[512,256]{1,0:T(8,128)(2,1)S(1)} fusion(bf16[512,2304]{1,0:T(8,128)(2,1)} %bitcast.55, bf16[2304,256]{1,0:T(8,128)(2,1)} %get-tuple-element.22), kind=kOutput, calls=%fused_computation.8 | convolution fusion | flops 604110848 | bytes 3801088 | tf_op jit(solution)/shard_map/dot_general | solution.py:156
  126.8 28.6 %all-gather.2 = bf16[1024,256]{1,0:T(8,128)(2,1)S(1)} all-gather(bf16[512,256]{1,0:T(8,128)(2,1)S(1)} %convolution_convert_fusion.1), channel_id=4, replica_groups=mesh['xh'=2,'z'=16,'xl'=2,'y'=4,'c'=2] {'xh'}, dimensions={0}, use_global_device_ids=true | all-gather | bytes 786432 | tf_op jit(solution)/shard_map/all_gather | solution.py:157
  155.5 0.1 multiply_subtract_fusion.1
  155.6 0.1 fusion.3
  155.8 0.7 pad_maximum_fusion.3.query_ref
  156.5 0.2 reshape.119
  156.7 13.5 %all-gather.9.cloned.1.call-done.kv_hbm = bf16[8192,256]{1,0:T(8,128)(2,1)} async-done(((bf16[512,256]{1,0:T(8,128)(2,1)}), bf16[8192,256]{1,0:T(8,128)(2,1)}) %all-gather.9.cloned.1.call-update) | async-done | bytes 4194320 | tf_op jit(solution)/shard_map/all_gather | solution.py:171
  170.2 9.9 %shard_map.82 = bf16[256,256]{1,0:T(8,128)(2,1)} custom-call(s32[3]{0:T(128)} %pad_add_fusion.where_ref, bf16[512,128]{1,0:T(8,128)(2,1)} %pad_maximum_fusion.3.query_ref, s32[512,1]{1,0:T(8,128)} %bitcast.60, bf16[8192,256]{1,0:T(8,128)(2,1)} %all-gather.9.cloned.1.call-done.kv_hbm), custom_call_target="tpu_custom_call" | custom-call | flops 1073741824 | bytes 2097152 | tf_op jit(solution)/shard_map/pallas_call | solution.py:88
  180.1 1.7 convolution_convert_fusion
  181.8 15.6 %all_to_all.46 = bf16[2,128,4608]{2,1,0:T(8,128)(2,1)S(1)} all-to-all(bf16[2,128,4608]{2,1,0:T(8,128)(2,1)S(1)} %bitcast.49), channel_id=1, replica_groups=mesh['xh'=2,'z'=16,'xl'=2,'y'=4,'c'=2] {'c'}, dimensions={0} | all-to-all | bytes 4718592 | tf_op jit(solution)/shard_map/all_to_all | solution.py:197
  197.5 0.3 add_convert_fusion
  197.7 20.5 %all_to_all.47 = bf16[8,16,4608]{2,1,0:T(8,128)(2,1)S(1)} all-to-all(bf16[8,16,4608]{2,1,0:T(8,128)(2,1)S(1)} %bitcast.53), channel_id=1, replica_groups=mesh['xh'=2,'z'=16,'xl'=2,'y'=4,'c'=2] {'xl','y'}, dimensions={0} | all-to-all | bytes 2359296 | tf_op jit(solution)/shard_map/all_to_all | solution.py:199
  218.3 0.2 convert_reduce_fusion
  218.4 0.2 multiply_reduce_fusion.1
  218.6 0.1 add_convert_fusion.1
  218.7 0.1 broadcast_in_dim.19
  218.8 18.1 %all_to_all.48 = bf16[8,16,4608]{2,1,0:T(8,128)(2,1)S(1)} all-to-all(bf16[8,16,4608]{2,1,0:T(8,128)(2,1)S(1)} %broadcast_in_dim.19), channel_id=1, replica_groups=mesh['xh'=2,'z'=16,'xl'=2,'y'=4,'c'=2] {'xl','y'}, dimensions={0} | all-to-all | bytes 2359296 | tf_op jit(solution)/shard_map/all_to_all | solution.py:24
  236.9 0.2 broadcast_in_dim.20
  237.0 8.2 %all_to_all.49 = bf16[2,128,4608]{2,1,0:T(8,128)(2,1)S(1)} all-to-all(bf16[2,128,4608]{2,1,0:T(8,128)(2,1)S(1)} %broadcast_in_dim.20), channel_id=1, replica_groups=mesh['xh'=2,'z'=16,'xl'=2,'y'=4,'c'=2] {'c'}, dimensions={0} | all-to-all | bytes 4718592 | tf_op jit(solution)/shard_map/all_to_all | solution.py:24
  245.2 1.4 copy.45
  (26 shorter events, 0.3 us)
Async XLA Ops:
  6.5 73.8 %all-gather.7.cloned.1.call-start = ((), (), s32[]{:S(2)}) async-start(), calls=%async_computation.9 | async-start | bytes 3760128 | tf_op jit(solution)/shard_map/all_gather | solution.py:117
  6.5 15.4 %copy-start.3 = (f32[4608]{0:T(1024)S(1)}, f32[4608]{0:T(1024)}, u32[]{:S(2)}) copy-start(f32[4608]{0:T(1024)} %param.10) | copy-start | bytes 55300
  9.8 6.8 %collective-permute-start = (bf16[304,256]{1,0:T(8,128)(2,1)S(1)}, bf16[304,256]{1,0:T(8,128)(2,1)S(1)}, u32[]{:S(2)}, u32[]{:S(2)}) collective-permute-start(bf16[304,256]{1,0:T(8,128)(2,1)S(1)} %pad_maximum_fusion.2), channel_id=1, source_target_pairs={{0,0},{8,256},{256,8},{264,264},{1,1},{9,257},{257,9},{265,265},{2... | collective-permute-start | bytes 466952 | tf_op jit(solution)/shard_map/ppermute | solution.py:122
  17.7 21.1 %all-to-all-start = ((bf16[8,1,304,256]{3,2,1,0:T(8,128)(2,1)}), bf16[8,1,304,256]{3,2,1,0:T(8,128)(2,1)S(1)}, u32[]{:S(2)}, u32[]{:S(2)}) async-start(bf16[8,1,304,256]{3,2,1,0:T(8,128)(2,1)} %broadcast_in_dim.15), calls=%async_computation | async-start | bytes 2490368 | tf_op jit(solution)/shard_map/all_to_all | solution.py:24
  46.2 25.0 %all-to-all-start.2 = ((f32[16,1,8]{2,1,0:T(1,128)}), f32[16,1,8]{2,1,0:T(1,128)S(1)}, u32[]{:S(2)}, u32[]{:S(2)}) async-start(f32[16,1,8]{2,1,0:T(1,128)} %broadcast_in_dim.17), calls=%async_computation.2 | async-start | bytes 16384 | tf_op jit(solution)/shard_map/all_to_all | solution.py:24
  60.9 109.3 %all-gather.9.cloned.1.call-start = ((), (), s32[]{:S(2)}) async-start(), calls=%async_computation.10 | async-start | bytes 4456448 | tf_op jit(solution)/shard_map/all_gather | solution.py:171
  80.3 3.0 %copy-start = (bf16[2,256,2304]{2,1,0:T(8,128)(2,1)S(1)}, bf16[2,256,2304]{2,1,0:T(8,128)(2,1)}, u32[]{:S(2)}) copy-start(bf16[2,256,2304]{2,1,0:T(8,128)(2,1)} %copy.31) | copy-start | bytes 7077892
  85.3 8.7 %copy-start.1 = (bf16[256,288]{0,1:T(8,128)(2,1)S(1)}, bf16[256,288]{0,1:T(8,128)(2,1)}, u32[]{:S(2)}) copy-start(bf16[256,288]{0,1:T(8,128)(2,1)} %param.8) | copy-start | bytes 442372
  94.9 23.1 %all-to-all-start.4 = ((bf16[16,16,288]{2,1,0:T(8,128)(2,1)}), bf16[16,16,288]{2,1,0:T(8,128)(2,1)S(1)}, u32[]{:S(2)}, u32[]{:S(2)}) async-start(bf16[16,16,288]{2,1,0:T(8,128)(2,1)} %bitcast.12), calls=%async_computation.4 | async-start | bytes 393216 | tf_op jit(solution)/shard_map/all_to_all | solution.py:189
  119.6 37.1 %all-to-all-start.3 = ((bf16[2,1,2304,256]{3,2,1,0:T(8,128)(2,1)}), bf16[2,1,2304,256]{3,2,1,0:T(8,128)(2,1)S(1)}, u32[]{:S(2)}, u32[]{:S(2)}) async-start(bf16[2,1,2304,256]{3,2,1,0:T(8,128)(2,1)} %broadcast_in_dim.18), calls=%async_computation.3 | async-start | bytes 4718592 | tf_op jit(solution)/shard_map/all_to_all | solution.py:24
  197.7 20.9 %copy-start.2 = (f32[4608]{0:T(1024)S(1)}, f32[4608]{0:T(1024)}, u32[]{:S(2)}) copy-start(f32[4608]{0:T(1024)} %param.11) | copy-start | bytes 55300
Sparse Core Ops, SparseCore 0:
  9.4 70.8 all-gather.6
  94.1 76.0 all-gather.8
